TPU v7x, 32 devices: a whole 2x2x4 slice. The times are simulated.
32 devices in a mesh: tile: 16 (over z, x, core), mem: 2 (over y).
Axes of the slice: x: 2, y: 2, z: 4, core: 2. Of those that a mesh axis runs over, the one named last changes fastest.
Arguments:
- anomalies: bfloat16 [80, 137, 2048], P('mem', None, 'tile'), may hold values from -6 to 6
- analysis_weights: bfloat16 [16, 80, 80], P('tile'), may hold values from -0.6 to 1.7
- background_mean: bfloat16 [137, 2048], P(None, 'tile'), may hold values from -6 to 6
- background: bfloat16 [80, 137, 2048], P('mem', None, 'tile'), may hold values from -6 to 6
- jacobian_table: bfloat16 [8461, 137], replicated, may hold values from -0.5 to 0.5
- channel_list: int32 [96], replicated, may hold values from 0 to 8460
- send_slots: int32 [16, 16, 32], P('tile'), may hold values from -1 to 127, as said below
- footprint: int32 [8192, 4], P('tile'), may hold values from 0 to 511, as said below
- footprint_weight: bfloat16 [8192, 4], P('tile'), may hold values from 0.25 to 1
- channel_bias: float32 [96], replicated, may hold values from -4 to 4
Outputs:
- analysis_members: bfloat16 [80, 137, 2048], P('mem', None, 'tile')
- radiance_prior: float32 [96, 80, 8192], P(None, 'mem', 'tile')
Inputs may be any that keep to these rules, and one draw needn't show every extreme that they name: `send_slots`: entry [s, d, i] is a column within owner s's block of 128 columns that owner s sends to tile d in slot i, or -1 for an empty slot; the filled slots of a pair come first, each pair fills 1 to 32 slots, and in every draw one tile receives 32 filled slots from every owner. `footprint`: entry [o, j] is a slot of the buffer of observation o's tile, which holds 32 slots from each owner in owner order; every entry names a filled slot, the 4 entries of a row differ, and every filled slot is named by some row of that tile.
All inputs are finite; a program needn't handle non-finite values.
Results may differ from a plain program's by a relative error of at most 0.0021.
Values may be sent and summed in bfloat16 or wider, within the bound.
A program may use at most 128 MiB of HBM per device.

v0:
```python
import functools

import jax
import jax.numpy as jnp
from jax import lax
from jax.experimental import pallas as pl
from jax.experimental.pallas import tpu as pltpu
from jax.sharding import PartitionSpec as P

LANES = 128
MESH = pl.DeviceIdType.MESH


def exchange_kernel(
    n,
    nm,
    owned_ref,
    target_ref,
    anom_ref,
    weight_ref,
    mean_ref,
    foot_ref,
    fweight_ref,
    recv_ref,
    analysis_ref,
    spread_ref,
    send_buf,
    relay_buf,
    relay_block,
    relay_target,
    pieces,
    mixed,
    spread,
    mean_wide,
    a_send,
    a_recv,
    m_send,
    m_recv,
    b_send,
    b_recv,
    r_send,
    local_sem,
):
    tile = lax.axis_index("tile")
    mem = lax.axis_index("mem")
    groups, rows, cols = owned_ref.shape
    chips = n // 2
    slots = spread_ref.shape[0] // n
    obs = spread_ref.shape[1]
    levels = anom_ref.shape[0]

    barrier = pltpu.get_barrier_semaphore()

    def greet(k, carry):
        pl.semaphore_signal(
            barrier, inc=1, device_id=(lax.rem(tile + k, n), mem), device_id_type=MESH
        )
        return carry

    lax.fori_loop(1, n, greet, 0)
    for k in range(1, nm):
        pl.semaphore_signal(
            barrier, inc=1, device_id=(tile, lax.rem(mem + k, nm)), device_id_type=MESH
        )
    own_piece = pltpu.make_async_copy(anom_ref, pieces.at[mem], local_sem.at[0])
    own_piece.start()
    pl.semaphore_wait(barrier, n - 1 + nm - 1)

    def member_copy(k):
        peer = lax.rem(mem + k, nm)
        return pltpu.make_async_remote_copy(
            src_ref=anom_ref,
            dst_ref=pieces.at[mem],
            send_sem=m_send.at[k],
            recv_sem=m_recv.at[k],
            device_id=(tile, peer),
            device_id_type=MESH,
        )

    for k in range(1, nm):
        member_copy(k).start()

    zone_tiles = n // 4
    zone_chips = chips // 4
    zone = tile // zone_tiles
    far_half = zone // 2
    near = zone - 3 * far_half
    depth = near * (1 - 2 * far_half)
    inner = depth == 1
    partner = lax.rem(tile + (1 - 2 * far_half) * zone_tiles + n, n)
    my_chip = tile // 2
    my_place = lax.rem(my_chip, zone_chips)
    halves = relay_split(rows)
    part = rows // halves

    def block_copies():
        for h in range(halves):
            span = (slice(None), pl.ds(h * part, part), slice(None))
            yield pltpu.make_async_remote_copy(
                src_ref=owned_ref.at[span],
                dst_ref=relay_block.at[span],
                send_sem=b_send.at[h],
                recv_sem=b_recv.at[h],
                device_id=(partner, mem),
                device_id_type=MESH,
            )
        yield pltpu.make_async_remote_copy(
            src_ref=target_ref,
            dst_ref=relay_target,
            send_sem=b_send.at[halves],
            recv_sem=b_recv.at[halves],
            device_id=(partner, mem),
            device_id_type=MESH,
        )

    @pl.when(inner)
    def _():
        for copy in reversed(list(block_copies())):
            copy.start()

    def tile_copy(dest):
        return pltpu.make_async_remote_copy(
            src_ref=send_buf.at[dest],
            dst_ref=recv_ref.at[tile],
            send_sem=a_send.at[dest],
            recv_sem=a_recv.at[tile],
            device_id=(dest, mem),
            device_id_type=MESH,
        )

    def relay_copy(h, dest):
        return pltpu.make_async_remote_copy(
            src_ref=relay_buf.at[dest, pl.ds(h * part, part)],
            dst_ref=recv_ref.at[partner, pl.ds(h * part, part)],
            send_sem=r_send.at[h, dest],
            recv_sem=a_recv.at[partner],
            device_id=(dest, mem),
            device_id_type=MESH,
        )

    def arrival(source):
        return pltpu.make_async_remote_copy(
            src_ref=send_buf.at[source],
            dst_ref=recv_ref.at[source],
            send_sem=a_send.at[source],
            recv_sem=a_recv.at[source],
            device_id=(source, mem),
            device_id_type=MESH,
        )

    def chip_of(their_zone, r):
        their_zone = their_zone + far_half * (3 - 2 * their_zone)
        return their_zone * zone_chips + lax.rem(my_place + r, zone_chips)

    def direct_chip(j):
        k = j // zone_chips
        outer_zone = k + (k // 2) * (5 - 2 * k)
        return chip_of(outer_zone + depth * (1 - k - outer_zone), lax.rem(j, zone_chips))

    row_id = lax.broadcasted_iota(jnp.int32, (groups * cols, 2 * LANES), 0)

    def pack(wide, table_ref, chip, out_ref, span):
        first = chip * 2
        want = jnp.concatenate([table_ref[first], table_ref[first + 1]], axis=1)
        pick = jnp.where(row_id == want, 1.0, 0.0).astype(jnp.bfloat16)
        out = jnp.dot(wide, pick, preferred_element_type=jnp.float32).astype(jnp.bfloat16)
        out_ref[first, span] = out[:, :LANES]
        out_ref[first + 1, span] = out[:, LANES:]

    def send(chip):
        for core in range(2):
            dest = chip * 2 + core

            @pl.when(dest != tile)
            def _():
                tile_copy(dest).start()

    wide = jnp.concatenate([owned_ref[g] for g in range(groups)], axis=1)
    whole = slice(None)
    pack(wide, target_ref, direct_chip(0), send_buf, whole)

    def step(j, carry):
        pack(wide, target_ref, direct_chip(j), send_buf, whole)
        send(direct_chip(j - 1))
        return carry

    steps = zone_chips * (4 - 2 * depth)
    lax.fori_loop(1, steps, step, 0)
    own_chunk = pltpu.make_async_copy(send_buf.at[tile], recv_ref.at[tile], local_sem.at[1])
    own_chunk.start()

    fweight = fweight_ref[...].astype(jnp.float32)

    def spread_rows(s, carry):
        ids = lax.broadcasted_iota(jnp.int32, (slots, obs), 0) + s * slots
        total = jnp.zeros((slots, obs), jnp.float32)
        for j in range(foot_ref.shape[0]):
            total = total + jnp.where(
                ids == foot_ref[j : j + 1, :], fweight[j : j + 1, :], 0.0
            )
        spread[pl.ds(pl.multiple_of(s * slots, slots), slots), :] = total.astype(jnp.bfloat16)
        return carry

    lax.fori_loop(0, n // 2, spread_rows, 0)
    send(direct_chip(steps - 1))

    def relay_chip(j):
        return chip_of(j // zone_chips, lax.rem(j, zone_chips))

    relay_own = pltpu.make_async_copy(relay_buf.at[tile], recv_ref.at[partner], local_sem.at[4])

    def relay_send(h, j):
        for core in range(2):
            dest = relay_chip(j) * 2 + core

            @pl.when(dest != tile)
            def _():
                relay_copy(h, dest).start()

    relay_steps = 2 * zone_chips

    @pl.when(inner)
    def _():
        copies = list(block_copies())
        copies[halves].wait()
        for h in range(halves):
            copies[h].wait()
            span = pl.ds(h * part, part)
            block = jnp.concatenate([relay_block[g, span] for g in range(groups)], axis=1)

            def relay_step(j, carry):
                pack(block, relay_target, relay_chip(j), relay_buf, span)

                @pl.when(j > 0)
                def _():
                    relay_send(h, j - 1)

                if h:

                    @pl.when(j == 0)
                    def _():
                        relay_send(h - 1, relay_steps - 1)

                return carry

            lax.fori_loop(0, relay_steps, relay_step, 0)

    lax.fori_loop(n // 2, n, spread_rows, 0)

    @pl.when(inner)
    def _():
        relay_send(halves - 1, relay_steps - 1)
        relay_own.start()

    own_piece.wait()
    spread_out = pltpu.make_async_copy(spread, spread_ref, local_sem.at[2])
    spread_out.start()
    for k in range(1, nm):
        member_copy(k).wait()

    mean_wide[...] = mean_ref[...].astype(jnp.float32)

    def mix(l, carry):
        total = jnp.broadcast_to(
            mean_wide[pl.ds(l, 1), :], (weight_ref.shape[1], cols)
        )
        mixture = jnp.zeros_like(total)
        for p in range(nm):
            mixture = mixture + jnp.dot(
                weight_ref[p], pieces[p, l], preferred_element_type=jnp.float32
            )
        mixed[l] = (total + mixture).astype(jnp.bfloat16)
        return carry

    lax.fori_loop(0, levels, mix, 0)

    analysis_out = pltpu.make_async_copy(mixed, analysis_ref, local_sem.at[3])
    analysis_out.start()

    def drain(k, carry):
        other = lax.rem(tile + k, n)
        same_half = (other // zone_tiles) // 2 == far_half

        @pl.when(jnp.logical_or(jnp.logical_not(inner), same_half))
        def _():
            tile_copy(other).wait_send()

        @pl.when(jnp.logical_and(inner, same_half))
        def _():
            for h in range(halves):
                relay_copy(h, other).wait_send()

        @pl.when(jnp.logical_not(jnp.logical_and(inner, other == partner)))
        def _():
            arrival(other).wait_recv()

        return carry

    lax.fori_loop(1, n, drain, 0)

    @pl.when(inner)
    def _():
        relay_own.wait()

    own_chunk.wait()
    spread_out.wait()
    analysis_out.wait()


def relay_split(rows):
    return 2 if rows % 32 == 0 else 1


def combine_kernel(n, groups, per_step, bias_ref, recv_ref, spread_ref, out_ref):
    step = pl.program_id(0)
    slots = spread_ref.shape[0] // n
    per_group = out_ref.shape[1] * pl.num_programs(0)
    members = out_ref.shape[2]
    rows = recv_ref.shape[1]
    blocks = [recv_ref[s] for s in range(n)]
    stacked = jnp.concatenate(
        [
            jnp.concatenate([block[:, g * slots : (g + 1) * slots] for block in blocks], axis=1)
            for g in range(groups)
        ],
        axis=0,
    )
    prior = jnp.dot(stacked, spread_ref[...], preferred_element_type=jnp.float32)
    for g in range(groups):
        for c in range(per_step):
            first = g * rows + c * members
            bias = bias_ref[g * per_group + step * per_step + c]
            out_ref[g, c] = prior[first : first + members, :] + bias


def shards(
    n,
    nm,
    anomalies,
    analysis_weights,
    background_mean,
    background,
    jacobian_table,
    channel_list,
    send_slots,
    footprint,
    footprint_weight,
    channel_bias,
):
    mem_dev, levels, cols = anomalies.shape
    channels = channel_list.shape[0]
    slots = send_slots.shape[2]
    obs = footprint.shape[0]
    groups = LANES // slots
    rows = channels * mem_dev // groups
    halves = relay_split(rows)
    mem = lax.axis_index("mem")

    chosen = (
        jnp.arange(jacobian_table.shape[0], dtype=jnp.int32)[:, None] == channel_list[None, :]
    ).astype(jnp.bfloat16)
    selected = jnp.einsum(
        "sl,sc->cl", jacobian_table, chosen, preferred_element_type=jnp.float32
    ).astype(jnp.bfloat16)
    owned = jnp.einsum(
        "cl,klx->ckx", selected, background, preferred_element_type=jnp.float32
    ).astype(jnp.bfloat16)
    owned = owned.reshape(groups, rows, cols)
    lane_rows = jnp.maximum(send_slots[0], 0)[:, None, :] + (
        jnp.arange(groups, dtype=jnp.int32) * cols
    )[None, :, None]
    target = lane_rows.reshape(n, 1, LANES)
    weights = lax.dynamic_slice_in_dim(analysis_weights[0], mem * mem_dev, mem_dev, 1)
    weights = jnp.transpose(weights.reshape(nm, mem_dev, mem_dev), (0, 2, 1))
    vmem = pl.BlockSpec(memory_space=pltpu.VMEM)
    hbm = pl.BlockSpec(memory_space=pl.ANY)
    received, analysis, spread = pl.pallas_call(
        functools.partial(exchange_kernel, n, nm),
        out_shape=(
            jax.ShapeDtypeStruct((n, rows, LANES), jnp.bfloat16),
            jax.ShapeDtypeStruct((levels, mem_dev, cols), jnp.bfloat16),
            jax.ShapeDtypeStruct((n * slots, obs), jnp.bfloat16),
        ),
        in_specs=[vmem, vmem, hbm, vmem, vmem, vmem, vmem],
        out_specs=(hbm, hbm, hbm),
        scratch_shapes=[
            pltpu.VMEM((n, rows, LANES), jnp.bfloat16),
            pltpu.VMEM((n, rows, LANES), jnp.bfloat16),
            pltpu.VMEM((groups, rows, cols), jnp.bfloat16),
            pltpu.VMEM((n, 1, LANES), jnp.int32),
            pltpu.VMEM((nm, levels, mem_dev, cols), jnp.bfloat16),
            pltpu.VMEM((levels, mem_dev, cols), jnp.bfloat16),
            pltpu.VMEM((n * slots, obs), jnp.bfloat16),
            pltpu.VMEM((levels, cols), jnp.float32),
            pltpu.SemaphoreType.DMA((n,)),
            pltpu.SemaphoreType.DMA((n,)),
            pltpu.SemaphoreType.DMA((nm,)),
            pltpu.SemaphoreType.DMA((nm,)),
            pltpu.SemaphoreType.DMA((halves + 1,)),
            pltpu.SemaphoreType.DMA((halves + 1,)),
            pltpu.SemaphoreType.DMA((halves, n)),
            pltpu.SemaphoreType.DMA((5,)),
        ],
        compiler_params=pltpu.CompilerParams(
            collective_id=0, has_side_effects=True, vmem_limit_bytes=24 * 1024 * 1024
        ),
        name="exchange",
    )(
        owned,
        target,
        jnp.transpose(anomalies, (1, 0, 2)),
        weights,
        background_mean,
        jnp.transpose(footprint),
        jnp.transpose(footprint_weight),
    )
    analysis_members = jnp.transpose(analysis, (1, 0, 2))

    per_group = channels // groups
    per_step = next(c for c in (4, 8, per_group) if c * mem_dev % 16 == 0)
    prior = pl.pallas_call(
        functools.partial(combine_kernel, n, groups, per_step),
        out_shape=jax.ShapeDtypeStruct((groups, per_group, mem_dev, obs), jnp.float32),
        grid=(per_group // per_step,),
        in_specs=[
            pl.BlockSpec(memory_space=pltpu.SMEM),
            pl.BlockSpec((n, per_step * mem_dev, LANES), lambda i: (0, i, 0)),
            pl.BlockSpec((n * slots, obs), lambda i: (0, 0)),
        ],
        out_specs=pl.BlockSpec((groups, per_step, mem_dev, obs), lambda i: (0, i, 0, 0)),
        compiler_params=pltpu.CompilerParams(vmem_limit_bytes=24 * 1024 * 1024),
        name="combine",
    )(channel_bias, received, spread)
    return analysis_members, prior.reshape(channels, mem_dev, obs)


def solution(mesh):
    placed = (
        P("mem", None, "tile"),
        P("tile", None, None),
        P(None, "tile"),
        P("mem", None, "tile"),
        P(),
        P(),
        P("tile", None, None),
        P("tile", None),
        P("tile", None),
        P(),
    )
    return jax.shard_map(
        functools.partial(shards, mesh.shape["tile"], mesh.shape["mem"]),
        mesh=mesh,
        in_specs=placed,
        out_specs=(P("mem", None, "tile"), P(None, "mem", "tile")),
        check_vma=False,
    )
```

profile of v0, /device:TPU:0, one launch (start us, length us, event | category | flops | bytes accessed | tf_op | source)
XLA Modules:
  0.0 87.4 jit_solution(4108473689298697173)
XLA Ops:
  0.6 0.0 copy-start
  0.7 0.1 add.31
  0.7 0.1 add.32
  0.8 0.8 maximum_bitcast_fusion
  1.7 0.8 constant_dynamic-slice_fusion
  2.5 0.1 copy.17
  2.6 0.1 add.30
  2.7 0.0 copy-done
  2.7 3.2 %fusion.4 = bf16[96,40,128]{2,0,1:T(8,128)(2,1)S(1)} fusion(bf16[40,137,128]{2,0,1:T(8,128)(2,1)} %param.13, bf16[8461,137]{0,1:T(8,128)(2,1)S(1)} %copy-done, s32[96]{0:T(128)} %param.15), kind=kOutput, calls=%fused_computation.5 | convolution fusion | flops 358551552 | bytes 4704618 | tf_op jit(solution)/shard_map/cl,klx->ckx/dot_general | solution.py:365
  5.9 0.0 copy-start.1
  5.9 0.0 copy-start.2
  5.9 0.0 copy-start.3
  5.9 0.0 copy-start.4
  5.9 0.0 copy-start.5
  6.0 0.4 copy.15
  6.3 0.9 %copy-done.1 = bf16[40,137,128]{2,0,1:T(8,128)(2,1)S(1)} copy-done((bf16[40,137,128]{2,0,1:T(8,128)(2,1)S(1)}, bf16[40,137,128]{2,0,1:T(8,128)(2,1)}, u32[]{:S(2)}) %copy-start.1) | copy-done | bytes 1402904
  7.2 0.0 copy-done.2
  7.3 0.0 copy-done.3
  7.3 0.0 copy-done.4
  7.3 72.3 %exchange.1 = (bf16[16,960,128]{2,1,0:T(8,128)(2,1)S(1)}, bf16[137,40,128]{2,1,0:T(8,128)(2,1)S(1)}, bf16[512,512]{1,0:T(8,128)(2,1)S(1)}) custom-call(bf16[4,960,128]{2,1,0:T(8,128)(2,1)S(1)} %bitcast.15, s32[16,1,128]{2,1,0:T(1,128)S(1)} %broadcast_add_fusion.target_ref, bf16[137,40,128]{2,1,0:T(8,128)(2,1)S(1)} %bitcast.16, ...), custom_call_target="tpu_custom_call" | custom-call | tf_op jit(solution)/shard_map/exchange/pallas_call | solution.py:377
  79.5 0.0 copy-done.5
  79.5 6.8 %combine.1 = f32[4,24,40,512]{3,2,1,0:T(8,128)} custom-call(f32[96]{0:T(128)S(1)} %copy-done.5, bf16[16,960,128]{2,1,0:T(8,128)(2,1)S(1)} %get-tuple-element.6.recv_ref, bf16[512,512]{1,0:T(8,128)(2,1)S(1)} %get-tuple-element.7.spread_ref), custom_call_target="tpu_custom_call" | custom-call | tf_op jit(solution)/shard_map/combine/pallas_call | solution.py:421
  86.4 1.1 %copy.25 = bf16[40,137,128]{2,0,1:T(8,128)(2,1)} copy(bf16[40,137,128]{2,0,1:T(8,128)(2,1)S(1)} %bitcast.17) | data formatting | bytes 2805760
  (3 shorter events, 0.0 us)
Async XLA Ops:
  0.6 2.0 %copy-start = (bf16[8461,137]{0,1:T(8,128)(2,1)S(1)}, bf16[8461,137]{0,1:T(8,128)(2,1)}, u32[]{:S(2)}) copy-start(bf16[8461,137]{0,1:T(8,128)(2,1)} %param.14) | copy-start | bytes 6954946
  5.9 1.4 %copy-start.1 = (bf16[40,137,128]{2,0,1:T(8,128)(2,1)S(1)}, bf16[40,137,128]{2,0,1:T(8,128)(2,1)}, u32[]{:S(2)}) copy-start(bf16[40,137,128]{2,0,1:T(8,128)(2,1)} %param.10) | copy-start | bytes 4208644
  5.9 1.3 %copy-start.2 = (bf16[137,128]{1,0:T(8,128)(2,1)S(1)}, bf16[137,128]{1,0:T(8,128)(2,1)}, u32[]{:S(2)}) copy-start(bf16[137,128]{1,0:T(8,128)(2,1)} %mean_ref.1) | copy-start | bytes 105220
  5.9 1.3 %copy-start.3 = (s32[512,4]{0,1:T(4,128)S(1)}, s32[512,4]{0,1:T(4,128)}, u32[]{:S(2)}) copy-start(s32[512,4]{0,1:T(4,128)} %param.17) | copy-start | bytes 24580
  5.9 1.3 %copy-start.4 = (bf16[512,4]{0,1:T(4,128)(2,1)S(1)}, bf16[512,4]{0,1:T(4,128)(2,1)}, u32[]{:S(2)}) copy-start(bf16[512,4]{0,1:T(4,128)(2,1)} %param.18) | copy-start | bytes 12292
  5.9 73.6 %copy-start.5 = (f32[96]{0:T(128)S(1)}, f32[96]{0:T(128)}, u32[]{:S(2)}) copy-start(f32[96]{0:T(128)} %bias_ref.1) | copy-start | bytes 1156
where the time goes:
time: 88.1 us; the launch traced here: 87.4 us
  Pallas kernels  79.1 us (90%)
  local copies, waits for them, and re-layouts  3.56 us (4%)
  matrix products  3.21 us (4%)
    pallas_call x1, Pallas kernels, shards(): pl.pallas_call(functools.partial(exchange_kernel, n, nm), out_shape=(jax....  72.3 us
    pallas_call x1, Pallas kernels, shards(): pl.pallas_call(functools.partial(combine_kernel, n, groups, per_step), ou...  6.82 us
    dot_general x1, matrix products, shards(): jnp.einsum('cl,klx->ckx', selected, background, preferred_element_type=jn...  3.21 us
    unnamed x13, local copies, waits for them, and re-layouts  2.03 us

commit v1 on v0

v1 whole, which is shorter than its diff:
```python
import functools

import jax
import jax.numpy as jnp
from jax import lax
from jax.experimental import pallas as pl
from jax.experimental.pallas import tpu as pltpu
from jax.sharding import PartitionSpec as P

LANES = 128
MESH = pl.DeviceIdType.MESH
ZONES = 4

OWN, OUTER, PARTNER, FAR = range(4)
NEAR_ZONE = (0, 1, 2, 3)
AWAY = {OWN: 4, PARTNER: 5, FAR: 6}


def exchange_kernel(
    n,
    nm,
    chunks,
    owned_ref,
    slots_ref,
    anom_ref,
    weight_ref,
    mean_ref,
    foot_ref,
    fweight_ref,
    recv_ref,
    analysis_ref,
    spread_ref,
    send_buf,
    block_buf,
    own_table,
    tables,
    picks,
    pieces,
    mixed,
    spread,
    mean_wide,
    weight_wide,
    stream_send,
    stream_recv,
    table_send,
    table_recv,
    m_send,
    m_recv,
    p_send,
    a_recv,
    local_sem,
):
    tile = lax.axis_index("tile")
    mem = lax.axis_index("mem")
    rows, cols = owned_ref.shape
    slots = slots_ref.shape[1]
    groups = LANES // slots
    obs = foot_ref.shape[1]
    levels, mem_dev = anom_ref.shape[0], anom_ref.shape[1]
    zone_tiles = n // ZONES
    pairs = zone_tiles // 2
    chunk = rows // chunks
    part = chunk // groups

    zone = tile // zone_tiles
    place = lax.rem(tile, zone_tiles)
    sign = 1 - 2 * (zone // 2)
    inner = jnp.logical_or(zone == 1, zone == 2)
    outer = jnp.logical_not(inner)
    stride = sign * zone_tiles
    ahead = lax.rem(tile + stride + n, n)
    source = (
        tile,
        lax.rem(tile - stride + n, n),
        ahead,
        lax.rem(tile + 2 * stride + n, n),
    )
    zone_base = zone * zone_tiles
    away_base = lax.rem(zone_base - stride + n, n)

    barrier = pltpu.get_barrier_semaphore()

    def greet(k, carry):
        pl.semaphore_signal(
            barrier, inc=1, device_id=(lax.rem(tile + k, n), mem), device_id_type=MESH
        )
        return carry

    lax.fori_loop(1, n, greet, 0)
    for k in range(1, nm):
        pl.semaphore_signal(
            barrier, inc=1, device_id=(tile, lax.rem(mem + k, nm)), device_id_type=MESH
        )
    own_piece = pltpu.make_async_copy(anom_ref, pieces.at[mem], local_sem.at[0])
    own_piece.start()

    columns = jnp.maximum(slots_ref[...], 0)
    own_table[...] = jnp.concatenate([columns + g * cols for g in range(groups)], axis=1)

    def build(table_ref, base, combo):
        row_id = lax.broadcasted_iota(jnp.int32, (groups * cols, 2 * LANES), 0)

        def pair(h, carry):
            first = base + 2 * h
            want = jnp.concatenate(
                [table_ref[pl.ds(first, 1), :], table_ref[pl.ds(first + 1, 1), :]], axis=1
            )
            picks[combo, h] = jnp.where(row_id == want, 1.0, 0.0).astype(jnp.bfloat16)
            return carry

        lax.fori_loop(0, pairs, pair, 0)

    build(own_table, zone_base, NEAR_ZONE[OWN])

    @pl.when(inner)
    def _():
        build(own_table, away_base, AWAY[OWN])

    pl.semaphore_wait(barrier, n - 1 + nm - 1)

    def span(c):
        return pl.ds(pl.multiple_of(c * chunk, chunk), chunk)

    def narrow(c):
        return pl.ds(pl.multiple_of(c * part, part), part)

    landing = jnp.where(inner, 1, 0)

    def own_stream(c):
        return pltpu.make_async_remote_copy(
            src_ref=owned_ref.at[span(c)],
            dst_ref=block_buf.at[landing, span(c)],
            send_sem=stream_send.at[0, c],
            recv_sem=stream_recv.at[landing, c],
            device_id=(ahead, mem),
            device_id_type=MESH,
        )

    def own_table_copy():
        return pltpu.make_async_remote_copy(
            src_ref=own_table,
            dst_ref=tables.at[landing],
            send_sem=table_send.at[0],
            recv_sem=table_recv.at[landing],
            device_id=(ahead, mem),
            device_id_type=MESH,
        )

    def forward_stream(c):
        return pltpu.make_async_remote_copy(
            src_ref=block_buf.at[0, span(c)],
            dst_ref=block_buf.at[2, span(c)],
            send_sem=stream_send.at[1, c],
            recv_sem=stream_recv.at[2, c],
            device_id=(ahead, mem),
            device_id_type=MESH,
        )

    def forward_table():
        return pltpu.make_async_remote_copy(
            src_ref=tables.at[0],
            dst_ref=tables.at[2],
            send_sem=table_send.at[1],
            recv_sem=table_recv.at[2],
            device_id=(ahead, mem),
            device_id_type=MESH,
        )

    def stream_arrival(block, c):
        return pltpu.make_async_remote_copy(
            src_ref=owned_ref.at[span(c)],
            dst_ref=block_buf.at[block - 1, span(c)],
            send_sem=stream_send.at[0, c],
            recv_sem=stream_recv.at[block - 1, c],
            device_id=(ahead, mem),
            device_id_type=MESH,
        )

    def table_arrival(block):
        return pltpu.make_async_remote_copy(
            src_ref=own_table,
            dst_ref=tables.at[block - 1],
            send_sem=table_send.at[0],
            recv_sem=table_recv.at[block - 1],
            device_id=(ahead, mem),
            device_id_type=MESH,
        )

    def member_copy(k):
        peer = lax.rem(mem + k, nm)
        return pltpu.make_async_remote_copy(
            src_ref=anom_ref,
            dst_ref=pieces.at[mem],
            send_sem=m_send.at[k],
            recv_sem=m_recv.at[k],
            device_id=(tile, peer),
            device_id_type=MESH,
        )

    def parcel(block, combo, base, t, rows_of):
        return pltpu.make_async_remote_copy(
            src_ref=send_buf.at[combo, t, rows_of],
            dst_ref=recv_ref.at[source[block], rows_of],
            send_sem=p_send.at[combo, t],
            recv_sem=a_recv.at[source[block]],
            device_id=(base + t, mem),
            device_id_type=MESH,
        )

    def pack(block, combo, c):
        block_ref = owned_ref if block == OWN else block_buf.at[block - 1]
        wide = jnp.concatenate(
            [
                block_ref[pl.ds(pl.multiple_of(c * chunk + g * part, part), part), :]
                for g in range(groups)
            ],
            axis=1,
        )

        def pair(h, carry):
            out = jnp.dot(wide, picks[combo, h], preferred_element_type=jnp.float32)
            out = out.astype(jnp.bfloat16)
            send_buf[combo, 2 * h, narrow(c)] = out[:, :LANES]
            send_buf[combo, 2 * h + 1, narrow(c)] = out[:, LANES:]
            return carry

        lax.fori_loop(0, pairs, pair, 0, unroll=pairs <= 2)

    def send(block, combo, base, c):
        def one(t, carry):
            @pl.when(base + t != tile)
            def _():
                parcel(block, combo, base, t, narrow(c)).start()

            return carry

        lax.fori_loop(0, zone_tiles, one, 0)

    def pack_near(block, c):
        pack(block, NEAR_ZONE[block], c)

    def send_near(block, c):
        send(block, NEAR_ZONE[block], zone_base, c)

    def pack_away(block, c):
        pack(block, AWAY[block], c)

    def send_away(block, c):
        send(block, AWAY[block], away_base, c)

    def keep(block):
        return pltpu.make_async_copy(
            send_buf.at[NEAR_ZONE[block], place], recv_ref.at[source[block]], local_sem.at[4 + block]
        )

    own_table_copy().start()

    def start_own(c, carry):
        own_stream(c).start()
        return carry

    lax.fori_loop(0, chunks, start_own, 0)

    @pl.when(inner)
    def _():
        def own_step(c, carry):
            pack_away(OWN, c)
            pack_near(OWN, c)
            send_away(OWN, c)

            @pl.when(c > 0)
            def _():
                send_near(OWN, c - 1)

            return carry

        lax.fori_loop(0, chunks, own_step, 0)

    @pl.when(outer)
    def _():
        def own_step(c, carry):
            pack_near(OWN, c)

            @pl.when(c > 0)
            def _():
                send_near(OWN, c - 1)

            return carry

        lax.fori_loop(0, chunks, own_step, 0)

    for k in range(1, nm):
        member_copy(k).start()

    @pl.when(inner)
    def _():
        table_arrival(OUTER).wait_recv()
        forward_table().start()
        build(tables.at[OUTER - 1], zone_base, NEAR_ZONE[OUTER])
        table_arrival(PARTNER).wait_recv()
        build(tables.at[PARTNER - 1], away_base, AWAY[PARTNER])
        build(tables.at[PARTNER - 1], zone_base, NEAR_ZONE[PARTNER])

    send_near(OWN, chunks - 1)
    keep(OWN).start()

    @pl.when(inner)
    def _():
        def mid_step(c, carry):
            stream_arrival(OUTER, c).wait_recv()
            forward_stream(c).start()
            stream_arrival(PARTNER, c).wait_recv()
            pack_away(PARTNER, c)
            pack_near(PARTNER, c)
            send_away(PARTNER, c)
            pack_near(OUTER, c)
            send_near(PARTNER, c)

            @pl.when(c > 0)
            def _():
                send_near(OUTER, c - 1)

            return carry

        lax.fori_loop(0, chunks, mid_step, 0)
        table_arrival(FAR).wait_recv()
        build(tables.at[FAR - 1], away_base, AWAY[FAR])
        build(tables.at[FAR - 1], zone_base, NEAR_ZONE[FAR])
        send_near(OUTER, chunks - 1)
        keep(OUTER).start()
        keep(PARTNER).start()

        def far_step(c, carry):
            stream_arrival(FAR, c).wait_recv()
            pack_away(FAR, c)
            pack_near(FAR, c)
            send_away(FAR, c)

            @pl.when(c > 0)
            def _():
                send_near(FAR, c - 1)

            return carry

        lax.fori_loop(0, chunks, far_step, 0)

    fweight = fweight_ref[...].astype(jnp.float32)

    def spread_rows(s, carry):
        ids = lax.broadcasted_iota(jnp.int32, (slots, obs), 0) + s * slots
        total = jnp.zeros((slots, obs), jnp.float32)
        for j in range(foot_ref.shape[0]):
            total = total + jnp.where(
                ids == foot_ref[j : j + 1, :], fweight[j : j + 1, :], 0.0
            )
        spread[pl.ds(pl.multiple_of(s * slots, slots), slots), :] = total.astype(jnp.bfloat16)
        return carry

    lax.fori_loop(0, n, spread_rows, 0)

    @pl.when(inner)
    def _():
        send_near(FAR, chunks - 1)
        keep(FAR).start()

    spread_out = pltpu.make_async_copy(spread, spread_ref, local_sem.at[2])
    spread_out.start()
    own_piece.wait()
    for k in range(1, nm):
        member_copy(k).wait()

    mean_wide[...] = mean_ref[...].astype(jnp.float32)
    weight_wide[...] = jnp.transpose(weight_ref[...].astype(jnp.float32))
    mine = weight_wide[pl.ds(mem * mem_dev, mem_dev), :].astype(jnp.bfloat16)
    shares = [mine[:, p * mem_dev : (p + 1) * mem_dev] for p in range(nm)]

    def mix(l, carry):
        total = jnp.broadcast_to(mean_wide[pl.ds(l, 1), :], (mem_dev, cols))
        mixture = jnp.zeros_like(total)
        for p in range(nm):
            mixture = mixture + jnp.dot(
                shares[p], pieces[p, l], preferred_element_type=jnp.float32
            )
        mixed[l] = (total + mixture).astype(jnp.bfloat16)
        return carry

    lax.fori_loop(0, levels, mix, 0)

    analysis_out = pltpu.make_async_copy(mixed, analysis_ref, local_sem.at[3])
    analysis_out.start()

    whole = pl.ds(0, rows // groups)

    def sent(block, combo, base):
        def one(t, carry):
            @pl.when(base + t != tile)
            def _():
                parcel(block, combo, base, t, whole).wait_send()

            return carry

        lax.fori_loop(0, zone_tiles, one, 0)

    def own_sent(c, carry):
        own_stream(c).wait_send()
        return carry

    lax.fori_loop(0, chunks, own_sent, 0)
    own_table_copy().wait_send()
    sent(OWN, NEAR_ZONE[OWN], zone_base)

    @pl.when(inner)
    def _():
        def forwarded(c, carry):
            forward_stream(c).wait_send()
            return carry

        lax.fori_loop(0, chunks, forwarded, 0)
        forward_table().wait_send()
        for block in (OUTER, PARTNER, FAR):
            sent(block, NEAR_ZONE[block], zone_base)
            keep(block).wait()
        for block in AWAY:
            sent(block, AWAY[block], away_base)

    def arrived(s, carry):
        here = jnp.logical_or(
            s == tile, jnp.logical_and(inner, lax.rem(s, zone_tiles) == place)
        )

        @pl.when(jnp.logical_not(here))
        def _():
            pltpu.make_async_remote_copy(
                src_ref=send_buf.at[0, 0],
                dst_ref=recv_ref.at[s],
                send_sem=p_send.at[0, 0],
                recv_sem=a_recv.at[s],
                device_id=(ahead, mem),
                device_id_type=MESH,
            ).wait_recv()

        return carry

    lax.fori_loop(0, n, arrived, 0)
    keep(OWN).wait()
    spread_out.wait()
    analysis_out.wait()


def combine_kernel(n, groups, bias_ref, recv_ref, spread_ref, out_ref):
    step = pl.program_id(0)
    slots = spread_ref.shape[0] // n
    channels, members = out_ref.shape[0], out_ref.shape[1]
    stacked = jnp.concatenate(
        [
            jnp.concatenate(
                [recv_ref[s, :, g * slots : (g + 1) * slots] for s in range(n)], axis=1
            )
            for g in range(groups)
        ],
        axis=0,
    )
    prior = jnp.dot(stacked, spread_ref[...], preferred_element_type=jnp.float32)
    for c in range(channels):
        bias = bias_ref[step * channels + c]
        out_ref[c] = prior[c * members : (c + 1) * members, :] + bias


def chunk_count(channels, mem_dev, groups):
    def fits(count):
        part = channels * mem_dev // (count * groups)
        return channels % count == 0 and part * count * groups == channels * mem_dev and part % 16 == 0

    return next(count for count in (6, 4, 3, 2, 1) if count == 1 or fits(count))


def shards(
    n,
    nm,
    anomalies,
    analysis_weights,
    background_mean,
    background,
    jacobian_table,
    channel_list,
    send_slots,
    footprint,
    footprint_weight,
    channel_bias,
):
    mem_dev, levels, cols = anomalies.shape
    channels = channel_list.shape[0]
    slots = send_slots.shape[2]
    obs, foot = footprint.shape
    groups = LANES // slots
    rows = channels * mem_dev
    members = analysis_weights.shape[1]
    chunks = chunk_count(channels, mem_dev, groups)
    zone_tiles = n // ZONES
    combos = len(NEAR_ZONE) + len(AWAY)

    chosen = (
        jnp.arange(jacobian_table.shape[0], dtype=jnp.int32)[:, None] == channel_list[None, :]
    ).astype(jnp.bfloat16)
    selected = jnp.einsum(
        "sl,sc->cl", jacobian_table, chosen, preferred_element_type=jnp.float32
    ).astype(jnp.bfloat16)
    owned = jnp.einsum(
        "cl,klx->ckx", selected, background, preferred_element_type=jnp.float32
    ).astype(jnp.bfloat16)
    vmem = pl.BlockSpec(memory_space=pltpu.VMEM)
    hbm = pl.BlockSpec(memory_space=pl.ANY)
    dma = pltpu.SemaphoreType.DMA
    received, analysis, spread = pl.pallas_call(
        functools.partial(exchange_kernel, n, nm, chunks),
        out_shape=(
            jax.ShapeDtypeStruct((n, rows // groups, LANES), jnp.bfloat16),
            jax.ShapeDtypeStruct((levels, mem_dev, cols), jnp.bfloat16),
            jax.ShapeDtypeStruct((n * slots, obs), jnp.bfloat16),
        ),
        in_specs=[vmem, vmem, hbm, vmem, vmem, vmem, vmem],
        out_specs=(hbm, hbm, hbm),
        scratch_shapes=[
            pltpu.VMEM((combos, zone_tiles, rows // groups, LANES), jnp.bfloat16),
            pltpu.VMEM((3, rows, cols), jnp.bfloat16),
            pltpu.VMEM((n, LANES), jnp.int32),
            pltpu.VMEM((3, n, LANES), jnp.int32),
            pltpu.VMEM((combos, zone_tiles // 2, groups * cols, 2 * LANES), jnp.bfloat16),
            pltpu.VMEM((nm, levels, mem_dev, cols), jnp.bfloat16),
            pltpu.VMEM((levels, mem_dev, cols), jnp.bfloat16),
            pltpu.VMEM((n * slots, obs), jnp.bfloat16),
            pltpu.VMEM((levels, cols), jnp.float32),
            pltpu.VMEM((members, members), jnp.float32),
            dma((2, chunks)),
            dma((3, chunks)),
            dma((2,)),
            dma((3,)),
            dma((nm,)),
            dma((nm,)),
            dma((combos, zone_tiles)),
            dma((n,)),
            dma((8,)),
        ],
        compiler_params=pltpu.CompilerParams(
            collective_id=0, has_side_effects=True, vmem_limit_bytes=40 * 1024 * 1024
        ),
        name="exchange",
    )(
        owned.reshape(rows, cols),
        send_slots[0],
        jnp.transpose(anomalies, (1, 0, 2)),
        analysis_weights[0],
        background_mean,
        jnp.transpose(footprint),
        jnp.transpose(footprint_weight),
    )
    analysis_members = jnp.transpose(analysis, (1, 0, 2))

    part = rows // (groups * chunks)
    prior = pl.pallas_call(
        functools.partial(combine_kernel, n, groups),
        out_shape=jax.ShapeDtypeStruct((channels, mem_dev, obs), jnp.float32),
        grid=(chunks,),
        in_specs=[
            pl.BlockSpec(memory_space=pltpu.SMEM),
            pl.BlockSpec((n, part, LANES), lambda i: (0, i, 0)),
            pl.BlockSpec((n * slots, obs), lambda i: (0, 0)),
        ],
        out_specs=pl.BlockSpec((channels // chunks, mem_dev, obs), lambda i: (i, 0, 0)),
        compiler_params=pltpu.CompilerParams(vmem_limit_bytes=24 * 1024 * 1024),
        name="combine",
    )(channel_bias, received, spread)
    return analysis_members, prior


def solution(mesh):
    placed = (
        P("mem", None, "tile"),
        P("tile", None, None),
        P(None, "tile"),
        P("mem", None, "tile"),
        P(),
        P(),
        P("tile", None, None),
        P("tile", None),
        P("tile", None),
        P(),
    )
    return jax.shard_map(
        functools.partial(shards, mesh.shape["tile"], mesh.shape["mem"]),
        mesh=mesh,
        in_specs=placed,
        out_specs=(P("mem", None, "tile"), P(None, "mem", "tile")),
        check_vma=False,
    )
```

time: 88.1 us -> 92.3 us (1.048)
  the two profiles are of different devices: /device:TPU:0 before, /device:TPU:12 now
where the time goes in v1:
time: 92.3 us; the launch traced here: 92.1 us
  Pallas kernels  84.1 us (91%)
  local copies, waits for them, and re-layouts  4.08 us (4%)
  matrix products  3.2 us (3%)
    pallas_call x1, Pallas kernels, shards(): pl.pallas_call(functools.partial(exchange_kernel, n, nm, chunks), out_sha...  77.3 us
    pallas_call x1, Pallas kernels, shards(): pl.pallas_call(functools.partial(combine_kernel, n, groups), out_shape=ja...  6.8 us
    unnamed x17, local copies, waits for them, and re-layouts  3.7 us
    dot_general x1, matrix products, shards(): jnp.einsum('cl,klx->ckx', selected, background, preferred_element_type=jn...  3.2 us

profile of v1, /device:TPU:12, one launch (start us, length us, event | category | flops | bytes accessed | tf_op | source)
XLA Modules:
  0.0 92.1 jit_solution(4758767454591992549)
XLA Ops:
  0.6 0.0 copy-start
  0.6 1.7 %copy-done = bf16[8461,137]{0,1:T(8,128)(2,1)S(1)} copy-done((bf16[8461,137]{0,1:T(8,128)(2,1)S(1)}, bf16[8461,137]{0,1:T(8,128)(2,1)}, u32[]{:S(2)}) %copy-start) | copy-done | bytes 2318338
  2.3 3.2 %fusion.4 = bf16[96,40,128]{2,0,1:T(8,128)(2,1)S(1)} fusion(bf16[40,137,128]{2,0,1:T(8,128)(2,1)} %param.13, bf16[8461,137]{0,1:T(8,128)(2,1)S(1)} %copy-done, s32[96]{0:T(128)} %param.15), kind=kOutput, calls=%fused_computation.5 | convolution fusion | flops 358551552 | bytes 4704618 | tf_op jit(solution)/shard_map/cl,klx->ckx/dot_general | solution.py:508
  5.5 0.0 copy-start.1
  5.6 0.0 copy-start.2
  5.6 0.0 copy-start.3
  5.6 0.0 copy-start.4
  5.6 0.0 copy-start.5
  5.6 0.0 copy-start.6
  5.6 0.0 copy-start.7
  5.6 0.4 copy.13
  6.0 0.9 copy-done.1
  6.9 0.0 copy-done.2
  6.9 0.0 copy-done.3
  6.9 0.0 copy-done.4
  6.9 0.0 copy-done.5
  6.9 0.0 copy-done.6
  6.9 77.3 %exchange.1 = (bf16[16,960,128]{2,1,0:T(8,128)(2,1)S(1)}, bf16[137,40,128]{2,1,0:T(8,128)(2,1)S(1)}, bf16[512,512]{1,0:T(8,128)(2,1)S(1)}) custom-call(bf16[3840,128]{1,0:T(8,128)(2,1)S(1)} %bitcast.12, s32[16,32]{1,0:T(8,128)S(1)} %bitcast.16, bf16[137,40,128]{2,1,0:T(8,128)(2,1)S(1)} %bitcast.13, bf16[80,80]{1,0:T(8,128)(2,1)S(1)} %bitcast.15, ...), custom_call_target="tpu_custom_call" | custom-call | tf_op jit(solution)/shard_map/exchange/pallas_call | solution.py:514
  84.2 0.0 copy-done.7
  84.2 6.8 %combine.1 = f32[96,40,512]{2,1,0:T(8,128)} custom-call(f32[96]{0:T(128)S(1)} %copy-done.7, bf16[16,960,128]{2,1,0:T(8,128)(2,1)S(1)} %get-tuple-element.6.recv_ref, bf16[512,512]{1,0:T(8,128)(2,1)S(1)} %get-tuple-element.7.spread_ref), custom_call_target="tpu_custom_call" | custom-call | tf_op jit(solution)/shard_map/combine/pallas_call | solution.py:560
  91.0 1.1 %copy.19 = bf16[40,137,128]{2,0,1:T(8,128)(2,1)} copy(bf16[40,137,128]{2,0,1:T(8,128)(2,1)S(1)} %bitcast.14) | data formatting | bytes 2805760
Async XLA Ops:
  0.6 1.7 %copy-start = (bf16[8461,137]{0,1:T(8,128)(2,1)S(1)}, bf16[8461,137]{0,1:T(8,128)(2,1)}, u32[]{:S(2)}) copy-start(bf16[8461,137]{0,1:T(8,128)(2,1)} %param.14) | copy-start | bytes 6954946
  5.5 1.4 %copy-start.1 = (bf16[40,137,128]{2,0,1:T(8,128)(2,1)S(1)}, bf16[40,137,128]{2,0,1:T(8,128)(2,1)}, u32[]{:S(2)}) copy-start(bf16[40,137,128]{2,0,1:T(8,128)(2,1)} %param.10) | copy-start | bytes 4208644
  5.6 1.3 %copy-start.2 = (bf16[137,128]{1,0:T(8,128)(2,1)S(1)}, bf16[137,128]{1,0:T(8,128)(2,1)}, u32[]{:S(2)}) copy-start(bf16[137,128]{1,0:T(8,128)(2,1)} %mean_ref.1) | copy-start | bytes 105220
  5.6 1.3 %copy-start.3 = (bf16[1,80,80]{2,1,0:T(8,128)(2,1)S(1)}, bf16[1,80,80]{2,1,0:T(8,128)(2,1)}, u32[]{:S(2)}) copy-start(bf16[1,80,80]{2,1,0:T(8,128)(2,1)} %param.11) | copy-start | bytes 38404
  5.6 1.3 %copy-start.4 = (s32[1,16,32]{2,1,0:T(8,128)S(1)}, s32[1,16,32]{2,1,0:T(8,128)}, u32[]{:S(2)}) copy-start(s32[1,16,32]{2,1,0:T(8,128)} %param.16) | copy-start | bytes 6148
  5.6 1.3 %copy-start.5 = (s32[512,4]{0,1:T(4,128)S(1)}, s32[512,4]{0,1:T(4,128)}, u32[]{:S(2)}) copy-start(s32[512,4]{0,1:T(4,128)} %param.17) | copy-start | bytes 24580
  5.6 1.3 %copy-start.6 = (bf16[512,4]{0,1:T(4,128)(2,1)S(1)}, bf16[512,4]{0,1:T(4,128)(2,1)}, u32[]{:S(2)}) copy-start(bf16[512,4]{0,1:T(4,128)(2,1)} %param.18) | copy-start | bytes 12292
  5.6 78.6 %copy-start.7 = (f32[96]{0:T(128)S(1)}, f32[96]{0:T(128)}, u32[]{:S(2)}) copy-start(f32[96]{0:T(128)} %bias_ref.1) | copy-start | bytes 1156

commit v2 on v1

--- a/solution.py
+++ b/solution.py
@@ -10,6 +10,7 @@
 LANES = 128
 MESH = pl.DeviceIdType.MESH
 ZONES = 4
+MIX_LEVELS = 8
 
 OWN, OUTER, PARTNER, FAR = range(4)
 NEAR_ZONE = (0, 1, 2, 3)
@@ -374,17 +375,23 @@
     mine = weight_wide[pl.ds(mem * mem_dev, mem_dev), :].astype(jnp.bfloat16)
     shares = [mine[:, p * mem_dev : (p + 1) * mem_dev] for p in range(nm)]
 
-    def mix(l, carry):
-        total = jnp.broadcast_to(mean_wide[pl.ds(l, 1), :], (mem_dev, cols))
-        mixture = jnp.zeros_like(total)
+    def mix(first, count):
+        mixture = jnp.zeros((mem_dev, count * cols), jnp.float32)
         for p in range(nm):
-            mixture = mixture + jnp.dot(
-                shares[p], pieces[p, l], preferred_element_type=jnp.float32
-            )
-        mixed[l] = (total + mixture).astype(jnp.bfloat16)
+            side = jnp.concatenate([pieces[p, first + i] for i in range(count)], axis=1)
+            mixture = mixture + jnp.dot(shares[p], side, preferred_element_type=jnp.float32)
+        for i in range(count):
+            total = mean_wide[pl.ds(first + i, 1), :] + mixture[:, i * cols : (i + 1) * cols]
+            mixed[first + i] = total.astype(jnp.bfloat16)
+
+    def mix_block(b, carry):
+        mix(b * MIX_LEVELS, MIX_LEVELS)
         return carry
 
-    lax.fori_loop(0, levels, mix, 0)
+    full = levels // MIX_LEVELS
+    lax.fori_loop(0, full, mix_block, 0)
+    if levels % MIX_LEVELS:
+        mix(full * MIX_LEVELS, levels % MIX_LEVELS)
 
     analysis_out = pltpu.make_async_copy(mixed, analysis_ref, local_sem.at[3])
     analysis_out.start()
@@ -447,8 +454,16 @@
     analysis_out.wait()
 
 
-def combine_kernel(n, groups, bias_ref, recv_ref, spread_ref, out_ref):
+def combine_kernel(
+    n, groups, bias_ref, recv_ref, spread_ref, mixed_ref, out_ref, analysis_ref, sem
+):
     step = pl.program_id(0)
+    carry_out = pltpu.make_async_copy(mixed_ref, analysis_ref, sem)
+
+    @pl.when(step == 0)
+    def _():
+        carry_out.start()
+
     slots = spread_ref.shape[0] // n
     channels, members = out_ref.shape[0], out_ref.shape[1]
     stacked = jnp.concatenate(
@@ -464,6 +479,10 @@
     for c in range(channels):
         bias = bias_ref[step * channels + c]
         out_ref[c] = prior[c * members : (c + 1) * members, :] + bias
+
+    @pl.when(step == pl.num_programs(0) - 1)
+    def _():
+        carry_out.wait()
 
 
 def chunk_count(channels, mem_dev, groups):
@@ -511,7 +530,7 @@
     vmem = pl.BlockSpec(memory_space=pltpu.VMEM)
     hbm = pl.BlockSpec(memory_space=pl.ANY)
     dma = pltpu.SemaphoreType.DMA
-    received, analysis, spread = pl.pallas_call(
+    received, mixed, spread = pl.pallas_call(
         functools.partial(exchange_kernel, n, nm, chunks),
         out_shape=(
             jax.ShapeDtypeStruct((n, rows // groups, LANES), jnp.bfloat16),
@@ -554,23 +573,29 @@
         jnp.transpose(footprint),
         jnp.transpose(footprint_weight),
     )
-    analysis_members = jnp.transpose(analysis, (1, 0, 2))
-
     part = rows // (groups * chunks)
-    prior = pl.pallas_call(
+    prior, analysis = pl.pallas_call(
         functools.partial(combine_kernel, n, groups),
-        out_shape=jax.ShapeDtypeStruct((channels, mem_dev, obs), jnp.float32),
+        out_shape=(
+            jax.ShapeDtypeStruct((channels, mem_dev, obs), jnp.float32),
+            jax.ShapeDtypeStruct(mixed.shape, mixed.dtype),
+        ),
         grid=(chunks,),
         in_specs=[
             pl.BlockSpec(memory_space=pltpu.SMEM),
             pl.BlockSpec((n, part, LANES), lambda i: (0, i, 0)),
             pl.BlockSpec((n * slots, obs), lambda i: (0, 0)),
+            vmem,
         ],
-        out_specs=pl.BlockSpec((channels // chunks, mem_dev, obs), lambda i: (i, 0, 0)),
+        out_specs=(
+            pl.BlockSpec((channels // chunks, mem_dev, obs), lambda i: (i, 0, 0)),
+            hbm,
+        ),
+        scratch_shapes=[dma],
         compiler_params=pltpu.CompilerParams(vmem_limit_bytes=24 * 1024 * 1024),
         name="combine",
-    )(channel_bias, received, spread)
-    return analysis_members, prior
+    )(channel_bias, received, spread, mixed)
+    return jnp.transpose(analysis, (1, 0, 2)), prior
 
 
 def solution(mesh):

time: 92.3 us -> 84.7 us (0.918)
  the two profiles are of different devices: /device:TPU:12 before, /device:TPU:0 now
where the time goes in v2:
time: 84.7 us; the launch traced here: 84 us
  Pallas kernels  77.1 us (91%)
  matrix products  3.2 us (4%)
  local copies, waits for them, and re-layouts  3 us (4%)
    pallas_call x1, Pallas kernels, shards(): pl.pallas_call(functools.partial(exchange_kernel, n, nm, chunks), out_sha...  70 us
    pallas_call x1, Pallas kernels, shards(): pl.pallas_call(functools.partial(combine_kernel, n, groups), out_shape=(j...  7.04 us
    dot_general x1, matrix products, shards(): jnp.einsum('cl,klx->ckx', selected, background, preferred_element_type=jn...  3.2 us
    unnamed x16, local copies, waits for them, and re-layouts  2.62 us

profile of v2, /device:TPU:0, one launch (start us, length us, event | category | flops | bytes accessed | tf_op | source)
XLA Modules:
  0.0 84.0 jit_solution(1906764986857397620)
XLA Ops:
  0.6 0.0 copy-start
  0.6 1.7 %copy-done = bf16[8461,137]{0,1:T(8,128)(2,1)S(1)} copy-done((bf16[8461,137]{0,1:T(8,128)(2,1)S(1)}, bf16[8461,137]{0,1:T(8,128)(2,1)}, u32[]{:S(2)}) %copy-start) | copy-done | bytes 2318338
  2.3 3.2 %fusion.4 = bf16[96,40,128]{2,0,1:T(8,128)(2,1)S(1)} fusion(bf16[40,137,128]{2,0,1:T(8,128)(2,1)} %param.13, bf16[8461,137]{0,1:T(8,128)(2,1)S(1)} %copy-done, s32[96]{0:T(128)} %param.15), kind=kOutput, calls=%fused_computation.5 | convolution fusion | flops 358551552 | bytes 4704618 | tf_op jit(solution)/shard_map/cl,klx->ckx/dot_general | solution.py:527
  5.5 0.0 copy-start.1
  5.6 0.0 copy-start.2
  5.6 0.0 copy-start.3
  5.6 0.0 copy-start.4
  5.6 0.0 copy-start.5
  5.6 0.0 copy-start.6
  5.6 0.0 copy-start.7
  5.6 0.4 copy.13
  6.0 0.9 %copy-done.1 = bf16[40,137,128]{2,0,1:T(8,128)(2,1)S(1)} copy-done((bf16[40,137,128]{2,0,1:T(8,128)(2,1)S(1)}, bf16[40,137,128]{2,0,1:T(8,128)(2,1)}, u32[]{:S(2)}) %copy-start.1) | copy-done | bytes 1402904
  6.9 0.0 copy-done.2
  6.9 0.0 copy-done.3
  6.9 0.0 copy-done.4
  6.9 0.0 copy-done.5
  6.9 0.0 copy-done.6
  6.9 70.0 %exchange.1 = (bf16[16,960,128]{2,1,0:T(8,128)(2,1)S(1)}, bf16[137,40,128]{2,1,0:T(8,128)(2,1)S(1)}, bf16[512,512]{1,0:T(8,128)(2,1)S(1)}) custom-call(bf16[3840,128]{1,0:T(8,128)(2,1)S(1)} %bitcast.12, s32[16,32]{1,0:T(8,128)S(1)} %bitcast.15, bf16[137,40,128]{2,1,0:T(8,128)(2,1)S(1)} %bitcast.13, bf16[80,80]{1,0:T(8,128)(2,1)S(1)} %bitcast.14, ...), custom_call_target="tpu_custom_call" | custom-call | tf_op jit(solution)/shard_map/exchange/pallas_call | solution.py:533
  76.9 0.0 copy-done.7
  77.0 7.0 %combine.1 = (f32[96,40,512]{2,1,0:T(8,128)}, bf16[137,40,128]{2,1,0:T(8,128)(2,1)}) custom-call(f32[96]{0:T(128)S(1)} %copy-done.7, bf16[16,960,128]{2,1,0:T(8,128)(2,1)S(1)} %get-tuple-element.7.recv_ref, bf16[512,512]{1,0:T(8,128)(2,1)S(1)} %get-tuple-element.8.spread_ref, bf16[137,40,128]{2,1,0:T(8,128)(2,1)S(1)} %get-tuple-element.9.mixed_ref), custom_call_target="tpu_custom_call" | custom-call | tf_op jit(solution)/shard_map/combine/pallas_call | solution.py:577
Async XLA Ops:
  0.6 1.7 %copy-start = (bf16[8461,137]{0,1:T(8,128)(2,1)S(1)}, bf16[8461,137]{0,1:T(8,128)(2,1)}, u32[]{:S(2)}) copy-start(bf16[8461,137]{0,1:T(8,128)(2,1)} %param.14) | copy-start | bytes 6954946
  5.5 1.4 %copy-start.1 = (bf16[40,137,128]{2,0,1:T(8,128)(2,1)S(1)}, bf16[40,137,128]{2,0,1:T(8,128)(2,1)}, u32[]{:S(2)}) copy-start(bf16[40,137,128]{2,0,1:T(8,128)(2,1)} %param.10) | copy-start | bytes 4208644
  5.6 1.3 %copy-start.2 = (bf16[137,128]{1,0:T(8,128)(2,1)S(1)}, bf16[137,128]{1,0:T(8,128)(2,1)}, u32[]{:S(2)}) copy-start(bf16[137,128]{1,0:T(8,128)(2,1)} %mean_ref.1) | copy-start | bytes 105220
  5.6 1.3 %copy-start.3 = (bf16[1,80,80]{2,1,0:T(8,128)(2,1)S(1)}, bf16[1,80,80]{2,1,0:T(8,128)(2,1)}, u32[]{:S(2)}) copy-start(bf16[1,80,80]{2,1,0:T(8,128)(2,1)} %param.11) | copy-start | bytes 38404
  5.6 1.3 %copy-start.4 = (s32[1,16,32]{2,1,0:T(8,128)S(1)}, s32[1,16,32]{2,1,0:T(8,128)}, u32[]{:S(2)}) copy-start(s32[1,16,32]{2,1,0:T(8,128)} %param.16) | copy-start | bytes 6148
  5.6 1.3 %copy-start.5 = (s32[512,4]{0,1:T(4,128)S(1)}, s32[512,4]{0,1:T(4,128)}, u32[]{:S(2)}) copy-start(s32[512,4]{0,1:T(4,128)} %param.17) | copy-start | bytes 24580
  5.6 1.3 %copy-start.6 = (bf16[512,4]{0,1:T(4,128)(2,1)S(1)}, bf16[512,4]{0,1:T(4,128)(2,1)}, u32[]{:S(2)}) copy-start(bf16[512,4]{0,1:T(4,128)(2,1)} %param.18) | copy-start | bytes 12292
  5.6 71.3 %copy-start.7 = (f32[96]{0:T(128)S(1)}, f32[96]{0:T(128)}, u32[]{:S(2)}) copy-start(f32[96]{0:T(128)} %bias_ref.1) | copy-start | bytes 1156

commit v3 on v2

v3 whole, which is shorter than its diff:
```python
import functools

import jax
import jax.numpy as jnp
from jax import lax
from jax.experimental import pallas as pl
from jax.experimental.pallas import tpu as pltpu
from jax.sharding import PartitionSpec as P

LANES = 128
MESH = pl.DeviceIdType.MESH
ZONES = 4
MIX_LEVELS = 8

OWN, OUTER, PARTNER, FAR = range(4)
AWAY = {OWN: 0, PARTNER: 1, FAR: 2}
CAP = 80
FOLD = 8


def needed(table_ref, source, base, count, cols):
    column = lax.broadcasted_iota(jnp.int32, (cols, LANES), 0)

    def one(t, hit):
        row = table_ref[source, pl.ds(base + t, 1), :]
        return jnp.where(column == row, 1.0, hit)

    hit = lax.fori_loop(0, count, one, jnp.zeros((cols, LANES), jnp.float32))
    return jnp.max(hit, axis=1, keepdims=True)


def positions(mask, cols):
    before = lax.broadcasted_iota(jnp.int32, (cols, cols), 1) < lax.broadcasted_iota(
        jnp.int32, (cols, cols), 0
    )
    full = jnp.broadcast_to(mask, (cols, LANES)).astype(jnp.bfloat16)
    return jnp.dot(
        jnp.where(before, 1.0, 0.0).astype(jnp.bfloat16), full, preferred_element_type=jnp.float32
    )


def front_kernel(
    n,
    select,
    *refs,
):
    if select:
        (table_ref, list_ref, field_ref, slots_ref, owned_ref, tables_ref, count_ref,
         message, gathered, counted, counts, table, field, wide, chosen, radiance,
         sends, arrives, local_sem) = refs
    else:
        (slots_ref, tables_ref, count_ref, message, gathered, counted, counts,
         sends, arrives, local_sem) = refs
    tile = lax.axis_index("tile")
    mem = lax.axis_index("mem")
    slots = slots_ref.shape[1]
    groups = LANES // slots
    cols = LANES
    zone_tiles = n // ZONES
    zone = tile // zone_tiles
    barrier = pltpu.get_barrier_semaphore()

    def greet(k, carry):
        pl.semaphore_signal(
            barrier, inc=1, device_id=(lax.rem(tile + k, n), mem), device_id_type=MESH
        )
        return carry

    lax.fori_loop(1, n, greet, 0)
    if select:
        load_table = pltpu.make_async_copy(table_ref, table, local_sem.at[0])
        load_table.start()
        load_field = pltpu.make_async_copy(field_ref, field, local_sem.at[1])
        load_field.start()

    message[0] = jnp.concatenate([slots_ref[...]] * groups, axis=1)
    most = jnp.zeros((1, 1), jnp.float32)
    for far in (0, ZONES - 1):
        mask = needed(message, 0, far * zone_tiles, zone_tiles, cols)
        total = jnp.sum(mask, axis=0, keepdims=True)
        most = jnp.maximum(most, jnp.where(zone == far, 0.0, total))
    counted[0] = jnp.broadcast_to(most, (1, LANES)).astype(jnp.int32)
    pl.semaphore_wait(barrier, n - 1)

    def tell(k, carry):
        pltpu.make_async_remote_copy(
            src_ref=counted.at[0],
            dst_ref=counts.at[tile],
            send_sem=sends.at[0],
            recv_sem=arrives.at[0],
            device_id=(lax.rem(tile + k, n), mem),
            device_id_type=MESH,
        ).start()
        return carry

    lax.fori_loop(1, n, tell, 0)
    for k in range(1, ZONES):
        pltpu.make_async_remote_copy(
            src_ref=message.at[0],
            dst_ref=gathered.at[zone],
            send_sem=sends.at[1],
            recv_sem=arrives.at[1],
            device_id=(lax.rem(tile + k * zone_tiles, n), mem),
            device_id_type=MESH,
        ).start()

    if select:
        spectrum = table_ref.shape[1]
        levels, mem_dev = field_ref.shape[0], field_ref.shape[1]
        channels = list_ref.shape[1]
        load_field.wait()
        wide[...] = field[...].astype(jnp.float32)
        load_table.wait()
        block = 11 * LANES
        total = jnp.zeros((levels, channels), jnp.float32)
        for first in range(0, spectrum, block):
            size = min(block, spectrum - first)
            entry = lax.broadcasted_iota(jnp.int32, (size, channels), 0) + first
            pick = jnp.where(entry == list_ref[...], 1.0, 0.0).astype(jnp.bfloat16)
            total = total + jnp.dot(
                table[:, first : first + size], pick, preferred_element_type=jnp.float32
            )
        chosen[...] = jnp.zeros_like(chosen)
        chosen[0:levels, 0:channels] = total
        picked = jnp.transpose(chosen[...])[:channels, :levels].astype(jnp.bfloat16)
        flat = wide.reshape(levels * mem_dev, cols)

        def member(k, carry):
            profile = flat[pl.ds(k, levels, stride=mem_dev), :].astype(jnp.bfloat16)
            radiance[pl.ds(k, channels, stride=mem_dev), :] = jnp.dot(
                picked, profile, preferred_element_type=jnp.float32
            )
            return carry

        lax.fori_loop(0, mem_dev, member, 0, unroll=8)
        owned_ref[...] = radiance[...].astype(jnp.bfloat16)

    counts[tile] = counted[0]
    gathered[zone] = message[0]

    def everyone(ref, count, kind):
        span = ref.at[pl.ds(0, count)]
        return pltpu.make_async_remote_copy(
            src_ref=span,
            dst_ref=span,
            send_sem=sends.at[kind],
            recv_sem=arrives.at[kind],
            device_id=(lax.rem(tile + 1, n), mem),
            device_id_type=MESH,
        )

    everyone(gathered, ZONES - 1, 1).wait_recv()
    tables_ref[...] = gathered[...]
    everyone(counts, n - 1, 0).wait_recv()

    def highest(s, top):
        return jnp.maximum(top, counts[s])

    top = lax.fori_loop(0, n, highest, jnp.zeros((1, LANES), jnp.int32))
    count_ref[0, 0] = jnp.max(top.astype(jnp.float32))
    everyone(counts, n - 1, 0).wait_send()
    everyone(gathered, ZONES - 1, 1).wait_send()


def exchange_kernel(
    n,
    nm,
    chunks,
    tight,
    owned_ref,
    tables_ref,
    anom_ref,
    weight_ref,
    mean_ref,
    foot_ref,
    fweight_ref,
    recv_ref,
    analysis_ref,
    spread_ref,
    send_buf,
    away_buf,
    block_buf,
    compact_buf,
    picks,
    away_picks,
    open_picks,
    pieces,
    mixed,
    spread,
    mean_wide,
    weight_wide,
    shares,
    stream_send,
    stream_recv,
    m_send,
    m_recv,
    p_send,
    away_send,
    away_recv,
    a_recv,
    local_sem,
):
    tile = lax.axis_index("tile")
    mem = lax.axis_index("mem")
    rows, cols = owned_ref.shape
    slots = spread_ref.shape[0] // n
    groups = LANES // slots
    obs = foot_ref.shape[1]
    levels, mem_dev = anom_ref.shape[0], anom_ref.shape[1]
    zone_tiles = n // ZONES
    pairs = zone_tiles // 2
    chunk = rows // chunks
    part = chunk // groups

    zone = tile // zone_tiles
    place = lax.rem(tile, zone_tiles)
    sign = 1 - 2 * (zone // 2)
    inner = jnp.logical_or(zone == 1, zone == 2)
    outer = jnp.logical_not(inner)
    stride = sign * zone_tiles
    ahead = lax.rem(tile + stride + n, n)

    def along(steps):
        return lax.rem(tile + steps * stride + ZONES * n, n)

    if tight:
        source = (tile, along(jnp.where(inner, -1, 1)), along(jnp.where(inner, 1, 2)),
                  along(jnp.where(inner, 2, 3)))
    else:
        source = (tile, along(-1), along(1), along(2))
    zone_base = zone * zone_tiles
    away_base = lax.rem(zone_base - stride + n, n)

    barrier = pltpu.get_barrier_semaphore()

    def greet(k, carry):
        pl.semaphore_signal(
            barrier,
            inc=1,
            device_id=(zone_base + lax.rem(place + k, zone_tiles), mem),
            device_id_type=MESH,
        )
        return carry

    lax.fori_loop(1, zone_tiles, greet, 0)
    for side in (-1, 1):

        @pl.when(jnp.logical_and(zone + side >= 0, zone + side < ZONES))
        def _():
            def greet_side(t, carry):
                pl.semaphore_signal(
                    barrier,
                    inc=1,
                    device_id=(zone_base + side * zone_tiles + t, mem),
                    device_id_type=MESH,
                )
                return carry

            lax.fori_loop(0, zone_tiles, greet_side, 0)

    for k in range(1, nm):
        pl.semaphore_signal(
            barrier, inc=1, device_id=(tile, lax.rem(mem + k, nm)), device_id_type=MESH
        )

    lane_group = lax.broadcasted_iota(jnp.int32, (1, LANES), 1) // slots

    def build(origin, base, into, first_pick):
        row_id = lax.broadcasted_iota(jnp.int32, (groups * cols, 2 * LANES), 0)

        def want(t):
            row = tables_ref[origin // zone_tiles, pl.ds(base + t, 1), :]
            return jnp.maximum(row, 0) + lane_group * cols

        def pair(h, carry):
            wants = jnp.concatenate([want(2 * h), want(2 * h + 1)], axis=1)
            into[first_pick, h] = jnp.where(row_id == wants, 1.0, 0.0).astype(jnp.bfloat16)
            return carry

        lax.fori_loop(0, pairs, pair, 0)

    def build_near(block):
        build(source[block], zone_base, picks, block)

    def build_away(block):
        origin = source[block]
        if not tight:
            build(origin, away_base, away_picks, AWAY[block])
            return
        mask = needed(tables_ref, origin // zone_tiles, away_base, zone_tiles, cols)
        place_of = positions(mask, cols)[:, 0:1].astype(jnp.int32)
        place_of = jnp.where(mask > 0.0, place_of, -FOLD * CAP)
        lane = lax.broadcasted_iota(jnp.int32, (cols, FOLD * CAP), 1)
        for g in range(FOLD):
            away_picks[AWAY[block], g * cols : (g + 1) * cols, :] = jnp.where(
                lane == place_of + g * CAP, 1.0, 0.0
            ).astype(jnp.bfloat16)

    def build_open(i):
        origin = source[1 + i]
        mask = needed(tables_ref, origin // zone_tiles, zone_base, zone_tiles, cols)
        column = lax.broadcasted_iota(jnp.int32, (cols, LANES), 0)
        row_id = lax.broadcasted_iota(jnp.int32, (FOLD * CAP, 2 * LANES), 0)

        def one(t, carry):
            row = tables_ref[origin // zone_tiles, pl.ds(zone_base + t, 1), :]
            ahead_of = jnp.where(column < row, mask, 0.0)
            spot = jnp.sum(ahead_of, axis=0, keepdims=True).astype(jnp.int32)
            wants = jnp.concatenate(
                [spot + (2 * lane_group + v) * CAP for v in range(2)], axis=1
            )
            open_picks[i, t] = jnp.where(row_id == wants, 1.0, 0.0).astype(jnp.bfloat16)
            return carry

        lax.fori_loop(0, zone_tiles, one, 0)

    build_near(OWN)

    @pl.when(inner)
    def _():
        build_away(OWN)

    greeted = zone_tiles - 1 + nm - 1 + jnp.where(inner, 2, 1) * zone_tiles
    pl.semaphore_wait(barrier, greeted)

    def span(c):
        return pl.ds(pl.multiple_of(c * chunk, chunk), chunk)

    def narrow(c):
        return pl.ds(pl.multiple_of(c * part, part), part)

    landing = jnp.where(inner, 1, 0)

    def own_stream(c):
        return pltpu.make_async_remote_copy(
            src_ref=owned_ref.at[span(c)],
            dst_ref=block_buf.at[landing, span(c)],
            send_sem=stream_send.at[0],
            recv_sem=stream_recv.at[landing, c],
            device_id=(ahead, mem),
            device_id_type=MESH,
        )

    def forward_stream(c):
        return pltpu.make_async_remote_copy(
            src_ref=block_buf.at[0, span(c)],
            dst_ref=block_buf.at[2, span(c)],
            send_sem=stream_send.at[1],
            recv_sem=stream_recv.at[2, c],
            device_id=(ahead, mem),
            device_id_type=MESH,
        )

    def stream_arrival(block, c):
        return pltpu.make_async_remote_copy(
            src_ref=owned_ref.at[span(c)],
            dst_ref=block_buf.at[block - 1, span(c)],
            send_sem=stream_send.at[0],
            recv_sem=stream_recv.at[block - 1, c],
            device_id=(ahead, mem),
            device_id_type=MESH,
        )

    def member_copy(k):
        peer = lax.rem(mem + k, nm)
        return pltpu.make_async_remote_copy(
            src_ref=anom_ref,
            dst_ref=pieces.at[nm - 1 - k],
            send_sem=m_send.at[k],
            recv_sem=m_recv.at[nm - k],
            device_id=(tile, peer),
            device_id_type=MESH,
        )

    def parcel(block, t, rows_of):
        return pltpu.make_async_remote_copy(
            src_ref=send_buf.at[block, t, rows_of],
            dst_ref=recv_ref.at[source[block], rows_of],
            send_sem=p_send.at[block],
            recv_sem=a_recv.at[0],
            device_id=(zone_base + t, mem),
            device_id_type=MESH,
        )

    def away_parcel(block, t, rows_of):
        return pltpu.make_async_remote_copy(
            src_ref=away_buf.at[AWAY[block], t, rows_of],
            dst_ref=recv_ref.at[source[block], rows_of],
            send_sem=away_send.at[AWAY[block]],
            recv_sem=a_recv.at[0],
            device_id=(away_base + t, mem),
            device_id_type=MESH,
        )

    fold_part = chunk // FOLD

    def folded(c):
        return pl.ds(pl.multiple_of(c * fold_part, fold_part), fold_part)

    def compact(i, c):
        return pltpu.make_async_remote_copy(
            src_ref=away_buf.at[i, folded(c)],
            dst_ref=compact_buf.at[i, folded(c)],
            send_sem=away_send.at[i],
            recv_sem=away_recv.at[i, c],
            device_id=(along(-1), mem),
            device_id_type=MESH,
        )

    def spread_out_rows(block, c, count, size):
        block_ref = owned_ref if block == OWN else block_buf.at[block - 1]
        return jnp.concatenate(
            [
                block_ref[pl.ds(pl.multiple_of(c * chunk + g * size, size), size), :]
                for g in range(count)
            ],
            axis=1,
        )

    def pack(block, c, pick_ref, pick, out_ref):
        wide = spread_out_rows(block, c, groups, part)

        def pair(h, carry):
            out = jnp.dot(wide, pick_ref[pick, h], preferred_element_type=jnp.float32)
            out = out.astype(jnp.bfloat16)
            out_ref[pick, 2 * h, narrow(c)] = out[:, :LANES]
            out_ref[pick, 2 * h + 1, narrow(c)] = out[:, LANES:]
            return carry

        lax.fori_loop(0, pairs, pair, 0, unroll=pairs <= 2)

    def pack_near(block, c):
        pack(block, c, picks, block, send_buf)

    def pack_away(block, c):
        if not tight:
            pack(block, c, away_picks, AWAY[block], away_buf)
            return
        wide = spread_out_rows(block, c, FOLD, fold_part)
        out = jnp.dot(wide, away_picks[AWAY[block]], preferred_element_type=jnp.float32)
        away_buf[AWAY[block], folded(c)] = out.astype(jnp.bfloat16)

    def unpack(i, c):
        held = compact_buf[i, folded(c)]

        def one(t, carry):
            out = jnp.dot(held, open_picks[i, t], preferred_element_type=jnp.float32)
            out = out.astype(jnp.bfloat16)
            for v in range(2):
                rows_of = pl.ds(
                    pl.multiple_of(c * part + v * fold_part, fold_part), fold_part
                )
                send_buf[1 + i, t, rows_of] = out[:, v * LANES : (v + 1) * LANES]
            return carry

        lax.fori_loop(0, zone_tiles, one, 0, unroll=zone_tiles <= 4)

    def send_near(block, c):
        def one(t, carry):
            @pl.when(zone_base + t != tile)
            def _():
                parcel(block, t, narrow(c)).start()

            return carry

        lax.fori_loop(0, zone_tiles, one, 0)

    def send_away(block, c):
        if tight:
            compact(AWAY[block], c).start()
            return

        def one(t, carry):
            away_parcel(block, t, narrow(c)).start()
            return carry

        lax.fori_loop(0, zone_tiles, one, 0)

    def keep(block):
        return pltpu.make_async_copy(
            send_buf.at[block, place], recv_ref.at[source[block]], local_sem.at[4 + block]
        )

    def start_own(c, carry):
        own_stream(c).start()
        return carry

    lax.fori_loop(0, chunks, start_own, 0)

    @pl.when(inner)
    def _():
        def own_step(c, carry):
            pack_away(OWN, c)
            pack_near(OWN, c)
            send_away(OWN, c)

            @pl.when(c > 0)
            def _():
                send_near(OWN, c - 1)

            return carry

        lax.fori_loop(0, chunks, own_step, 0)

    @pl.when(outer)
    def _():
        def own_step(c, carry):
            pack_near(OWN, c)

            @pl.when(c > 0)
            def _():
                send_near(OWN, c - 1)

            return carry

        lax.fori_loop(0, chunks, own_step, 0)

    for k in range(1, nm):
        member_copy(k).start()

    @pl.when(inner)
    def _():
        build_away(PARTNER)
        build_near(PARTNER)
        build_near(OUTER)

    send_near(OWN, chunks - 1)
    keep(OWN).start()

    @pl.when(inner)
    def _():
        def mid_step(c, carry):
            stream_arrival(OUTER, c).wait_recv()
            forward_stream(c).start()
            stream_arrival(PARTNER, c).wait_recv()
            pack_away(PARTNER, c)
            pack_near(PARTNER, c)
            send_away(PARTNER, c)
            pack_near(OUTER, c)
            send_near(PARTNER, c)

            @pl.when(c > 0)
            def _():
                send_near(OUTER, c - 1)

            return carry

        lax.fori_loop(0, chunks, mid_step, 0)
        build_away(FAR)
        build_near(FAR)
        send_near(OUTER, chunks - 1)
        keep(OUTER).start()
        keep(PARTNER).start()

        def far_step(c, carry):
            stream_arrival(FAR, c).wait_recv()
            pack_away(FAR, c)
            pack_near(FAR, c)
            send_away(FAR, c)

            @pl.when(c > 0)
            def _():
                send_near(FAR, c - 1)

            return carry

        lax.fori_loop(0, chunks, far_step, 0)

    fweight = fweight_ref[...].astype(jnp.float32)

    def spread_rows(s, carry):
        ids = lax.broadcasted_iota(jnp.int32, (slots, obs), 0) + s * slots
        total = jnp.zeros((slots, obs), jnp.float32)
        for j in range(foot_ref.shape[0]):
            total = total + jnp.where(
                ids == foot_ref[j : j + 1, :], fweight[j : j + 1, :], 0.0
            )
        spread[pl.ds(pl.multiple_of(s * slots, slots), slots), :] = total.astype(jnp.bfloat16)
        return carry

    if tight:

        @pl.when(outer)
        def _():
            for i in range(3):
                build_open(i)

    lax.fori_loop(0, n, spread_rows, 0)

    @pl.when(inner)
    def _():
        send_near(FAR, chunks - 1)
        keep(FAR).start()

    if tight:

        def open_compact(i):
            def step(c, carry):
                compact(i, c).wait_recv()
                unpack(i, c)

                @pl.when(c > 0)
                def _():
                    send_near(1 + i, c - 1)

                return carry

            lax.fori_loop(0, chunks, step, 0)

        @pl.when(outer)
        def _():
            open_compact(0)
            send_near(1, chunks - 1)
            keep(1).start()
            open_compact(1)
            send_near(2, chunks - 1)
            keep(2).start()

    spread_out = pltpu.make_async_copy(spread, spread_ref, local_sem.at[2])
    spread_out.start()
    for k in range(1, nm):
        pltpu.make_async_remote_copy(
            src_ref=anom_ref,
            dst_ref=pieces.at[k - 1],
            send_sem=m_send.at[k],
            recv_sem=m_recv.at[k],
            device_id=(tile, lax.rem(mem + k, nm)),
            device_id_type=MESH,
        ).wait()

    mean_wide[...] = mean_ref[...].astype(jnp.float32)
    weight_wide[...] = jnp.transpose(weight_ref[...].astype(jnp.float32))
    mine = weight_wide[pl.ds(mem * mem_dev, mem_dev), :].astype(jnp.bfloat16)
    for p in range(nm):
        shares[p] = mine[:, p * mem_dev : (p + 1) * mem_dev]

    def mix(first, count):
        mixture = jnp.zeros((mem_dev, count * cols), jnp.float32)
        for k in range(nm):
            held = anom_ref if k == 0 else pieces.at[k - 1]
            side = jnp.concatenate([held[first + i] for i in range(count)], axis=1)
            share = shares[lax.rem(mem + k, nm)]
            mixture = mixture + jnp.dot(share, side, preferred_element_type=jnp.float32)
        for i in range(count):
            total = mean_wide[pl.ds(first + i, 1), :] + mixture[:, i * cols : (i + 1) * cols]
            mixed[first + i] = total.astype(jnp.bfloat16)

    def mix_block(b, carry):
        mix(b * MIX_LEVELS, MIX_LEVELS)
        return carry

    full = levels // MIX_LEVELS
    lax.fori_loop(0, full, mix_block, 0)
    if levels % MIX_LEVELS:
        mix(full * MIX_LEVELS, levels % MIX_LEVELS)

    analysis_out = pltpu.make_async_copy(mixed, analysis_ref, local_sem.at[3])
    analysis_out.start()

    if tight:

        @pl.when(outer)
        def _():
            open_compact(2)
            send_near(3, chunks - 1)
            keep(3).start()

    def gone(ref, sem):
        pltpu.make_async_remote_copy(
            src_ref=ref,
            dst_ref=ref,
            send_sem=sem,
            recv_sem=a_recv.at[0],
            device_id=(ahead, mem),
            device_id_type=MESH,
        ).wait_send()

    def come(count):
        pltpu.make_async_remote_copy(
            src_ref=recv_ref.at[pl.ds(0, count)],
            dst_ref=recv_ref.at[pl.ds(0, count)],
            send_sem=p_send.at[0],
            recv_sem=a_recv.at[0],
            device_id=(ahead, mem),
            device_id_type=MESH,
        ).wait_recv()

    gone(owned_ref, stream_send.at[0])
    gone(send_buf.at[OWN, pl.ds(0, zone_tiles - 1)], p_send.at[OWN])

    def line_sent():
        for block in (OUTER, PARTNER, FAR):
            gone(send_buf.at[block, pl.ds(0, zone_tiles - 1)], p_send.at[block])
            keep(block).wait()

    @pl.when(inner)
    def _():
        gone(block_buf.at[0], stream_send.at[1])
        for block in AWAY:
            gone(away_buf.at[AWAY[block]], away_send.at[AWAY[block]])
        line_sent()

    @pl.when(outer)
    def _():
        if tight:
            line_sent()
            come(n - ZONES)
        else:
            come(n - 1)

    @pl.when(inner)
    def _():
        come(n - ZONES)

    keep(OWN).wait()
    spread_out.wait()
    analysis_out.wait()


def combine_kernel(
    n, groups, bias_ref, recv_ref, spread_ref, mixed_ref, out_ref, analysis_ref, sem
):
    step = pl.program_id(0)
    carry_out = pltpu.make_async_copy(mixed_ref, analysis_ref, sem)

    @pl.when(step == 0)
    def _():
        carry_out.start()

    slots = spread_ref.shape[0] // n
    channels, members = out_ref.shape[0], out_ref.shape[1]
    stacked = jnp.concatenate(
        [
            jnp.concatenate(
                [recv_ref[s, :, g * slots : (g + 1) * slots] for s in range(n)], axis=1
            )
            for g in range(groups)
        ],
        axis=0,
    )
    prior = jnp.dot(stacked, spread_ref[...], preferred_element_type=jnp.float32)
    for c in range(channels):
        bias = bias_ref[step * channels + c]
        out_ref[c] = prior[c * members : (c + 1) * members, :] + bias

    @pl.when(step == pl.num_programs(0) - 1)
    def _():
        carry_out.wait()


def chunk_count(channels, mem_dev, groups):
    def fits(count):
        part = channels * mem_dev // (count * groups)
        return channels % count == 0 and part * count * groups == channels * mem_dev and part % 16 == 0

    return next(count for count in (6, 4, 3, 2, 1) if count == 1 or fits(count))


def shards(
    n,
    nm,
    anomalies,
    analysis_weights,
    background_mean,
    background,
    jacobian_table,
    channel_list,
    send_slots,
    footprint,
    footprint_weight,
    channel_bias,
):
    mem_dev, levels, cols = anomalies.shape
    channels = channel_list.shape[0]
    slots = send_slots.shape[2]
    obs, foot = footprint.shape
    groups = LANES // slots
    rows = channels * mem_dev
    members = analysis_weights.shape[1]
    chunks = chunk_count(channels, mem_dev, groups)
    zone_tiles = n // ZONES
    vmem = pl.BlockSpec(memory_space=pltpu.VMEM)
    hbm = pl.BlockSpec(memory_space=pl.ANY)
    far = pl.BlockSpec(memory_space=pltpu.HBM)
    dma = pltpu.SemaphoreType.DMA
    chunk = rows // chunks
    select = mem_dev % 8 == 0
    foldable = chunk % (16 * FOLD) == 0

    front_out = [
        jax.ShapeDtypeStruct((ZONES, n, LANES), jnp.int32),
        jax.ShapeDtypeStruct((1, 1), jnp.float32),
    ]
    front_scratch = [
        pltpu.VMEM((1, n, LANES), jnp.int32),
        pltpu.VMEM((ZONES, n, LANES), jnp.int32),
        pltpu.VMEM((1, 1, LANES), jnp.int32),
        pltpu.VMEM((n, 1, LANES), jnp.int32),
    ]
    front_args, front_specs = [send_slots[0]], [vmem]
    if select:
        spectrum = jacobian_table.shape[0]
        front_out.insert(0, jax.ShapeDtypeStruct((rows, cols), jnp.bfloat16))
        front_scratch += [
            pltpu.VMEM((levels, spectrum), jnp.bfloat16),
            pltpu.VMEM((levels, mem_dev, cols), jnp.bfloat16),
            pltpu.VMEM((levels, mem_dev, cols), jnp.float32),
            pltpu.VMEM((-(-levels // LANES) * LANES, -(-channels // LANES) * LANES), jnp.float32),
            pltpu.VMEM((rows, cols), jnp.float32),
        ]
        front_args = [
            jnp.transpose(jacobian_table),
            channel_list[None, :],
            jnp.transpose(background, (1, 0, 2)),
            send_slots[0],
        ]
        front_specs = [far, vmem, far, vmem]
    front = pl.pallas_call(
        functools.partial(front_kernel, n, select),
        out_shape=tuple(front_out),
        in_specs=front_specs,
        out_specs=(vmem,) * (len(front_out) - 1) + (pl.BlockSpec(memory_space=pltpu.SMEM),),
        scratch_shapes=front_scratch + [dma((2,)), dma((2,)), dma((2,))],
        compiler_params=pltpu.CompilerParams(
            collective_id=0, has_side_effects=True, vmem_limit_bytes=62 * 1024 * 1024
        ),
        name="front",
    )(*front_args)
    tables, count = front[-2:]
    if select:
        owned = front[0]
    else:
        chosen = (
            jnp.arange(jacobian_table.shape[0], dtype=jnp.int32)[:, None] == channel_list[None, :]
        ).astype(jnp.bfloat16)
        selected = jnp.einsum(
            "sl,sc->cl", jacobian_table, chosen, preferred_element_type=jnp.float32
        ).astype(jnp.bfloat16)
        owned = jnp.einsum(
            "cl,klx->ckx", selected, background, preferred_element_type=jnp.float32
        ).astype(jnp.bfloat16).reshape(rows, cols)

    def rest(tight, owned, tables, anomalies, weights, mean, footprint, footprint_weight, bias):
        part = rows // groups
        if tight:
            variant = [
                pltpu.VMEM((3, rows // FOLD, FOLD * CAP), jnp.bfloat16),
                pltpu.VMEM((3, rows, cols), jnp.bfloat16),
                pltpu.VMEM((3, rows // FOLD, FOLD * CAP), jnp.bfloat16),
                pltpu.VMEM((4, zone_tiles // 2, groups * cols, 2 * LANES), jnp.bfloat16),
                pltpu.VMEM((3, FOLD * cols, FOLD * CAP), jnp.bfloat16),
                pltpu.VMEM((3, zone_tiles, FOLD * CAP, 2 * LANES), jnp.bfloat16),
            ]
        else:
            spare = pltpu.VMEM((8, LANES), jnp.bfloat16)
            variant = [
                pltpu.VMEM((3, zone_tiles, part, LANES), jnp.bfloat16),
                pltpu.VMEM((3, rows, cols), jnp.bfloat16),
                spare,
                pltpu.VMEM((4, zone_tiles // 2, groups * cols, 2 * LANES), jnp.bfloat16),
                pltpu.VMEM((3, zone_tiles // 2, groups * cols, 2 * LANES), jnp.bfloat16),
                spare,
            ]
        received, mixed, spread = pl.pallas_call(
            functools.partial(exchange_kernel, n, nm, chunks, tight),
            out_shape=(
                jax.ShapeDtypeStruct((n, part, LANES), jnp.bfloat16),
                jax.ShapeDtypeStruct((levels, mem_dev, cols), jnp.bfloat16),
                jax.ShapeDtypeStruct((n * slots, obs), jnp.bfloat16),
            ),
            in_specs=[vmem] * 7,
            out_specs=(hbm, hbm, hbm),
            scratch_shapes=[pltpu.VMEM((4, zone_tiles, part, LANES), jnp.bfloat16)]
            + variant
            + [
                pltpu.VMEM((max(nm - 1, 1), levels, mem_dev, cols), jnp.bfloat16),
                pltpu.VMEM((levels, mem_dev, cols), jnp.bfloat16),
                pltpu.VMEM((n * slots, obs), jnp.bfloat16),
                pltpu.VMEM((levels, cols), jnp.float32),
                pltpu.VMEM((members, members), jnp.float32),
                pltpu.VMEM((nm, mem_dev, mem_dev), jnp.bfloat16),
                dma((2,)),
                dma((3, chunks)),
                dma((nm,)),
                dma((nm,)),
                dma((4,)),
                dma((3,)),
                dma((3, chunks)),
                dma((1,)),
                dma((8,)),
            ],
            compiler_params=pltpu.CompilerParams(
                collective_id=1 + tight, has_side_effects=True, vmem_limit_bytes=44 * 1024 * 1024
            ),
            name="exchange_tight" if tight else "exchange",
        )(owned, tables, anomalies, weights, mean, footprint, footprint_weight)
        return pl.pallas_call(
            functools.partial(combine_kernel, n, groups),
            out_shape=(
                jax.ShapeDtypeStruct((channels, mem_dev, obs), jnp.float32),
                jax.ShapeDtypeStruct(mixed.shape, mixed.dtype),
            ),
            grid=(chunks,),
            in_specs=[
                pl.BlockSpec(memory_space=pltpu.SMEM),
                pl.BlockSpec((n, part // chunks, LANES), lambda i: (0, i, 0)),
                pl.BlockSpec((n * slots, obs), lambda i: (0, 0)),
                vmem,
            ],
            out_specs=(
                pl.BlockSpec((channels // chunks, mem_dev, obs), lambda i: (i, 0, 0)),
                hbm,
            ),
            scratch_shapes=[dma],
            compiler_params=pltpu.CompilerParams(vmem_limit_bytes=24 * 1024 * 1024),
            name="combine",
        )(bias, received, spread, mixed)

    operands = (
        owned,
        tables,
        jnp.transpose(anomalies, (1, 0, 2)),
        analysis_weights[0],
        background_mean,
        jnp.transpose(footprint),
        jnp.transpose(footprint_weight),
        channel_bias,
    )
    if foldable:
        prior, analysis = lax.cond(
            count[0, 0] <= CAP,
            functools.partial(rest, True),
            functools.partial(rest, False),
            *operands,
        )
    else:
        prior, analysis = rest(False, *operands)
    return jnp.transpose(analysis, (1, 0, 2)), prior


def solution(mesh):
    placed = (
        P("mem", None, "tile"),
        P("tile", None, None),
        P(None, "tile"),
        P("mem", None, "tile"),
        P(),
        P(),
        P("tile", None, None),
        P("tile", None),
        P("tile", None),
        P(),
    )
    return jax.shard_map(
        functools.partial(shards, mesh.shape["tile"], mesh.shape["mem"]),
        mesh=mesh,
        in_specs=placed,
        out_specs=(P("mem", None, "tile"), P(None, "mem", "tile")),
        check_vma=False,
    )
```

time: 84.7 us -> 76.2 us (0.90)
  matrix products: 3.2 us -> 0 us
  local copies, waits for them, and re-layouts: 3 us -> 0.03 us
  Pallas kernels: 77.1 us -> 74.5 us
    dot_general x1 -> x0, matrix products: 3.2 us -> none  [shards(): jnp.einsum('cl,klx->ckx', selected, background, preferred_element_type=jn...]
    unnamed x16 -> x12, local copies, waits for them, and re-layouts: 2.62 us -> 0.03 us
    pallas_call x2 -> x3, Pallas kernels: 77.1 us -> 74.5 us  [the longest x1 56.8 us: rest(): pl.pallas_call(functools.partial(exchange_kernel, n, nm, chunks, tight),...]
where the time goes in v3:
time: 76.2 us; the launch traced here: 75.9 us
  Pallas kernels  74.5 us (98%)
  between operations  1.36 us (2%)
    pallas_call x1, Pallas kernels, rest(): pl.pallas_call(functools.partial(exchange_kernel, n, nm, chunks, tight),...  56.8 us
    pallas_call x1, Pallas kernels, shards(): pl.pallas_call(functools.partial(front_kernel, n, select), out_shape=tupl...  10.7 us
    pallas_call x1, Pallas kernels, rest(): pl.pallas_call(functools.partial(combine_kernel, n, groups), out_shape=(j...  7.02 us

profile of v3, /device:TPU:0, one launch (start us, length us, event | category | flops | bytes accessed | tf_op | source)
XLA Modules:
  0.0 75.9 jit_solution(6154997380499418837)
XLA Ops:
  0.6 0.0 copy-start
  0.6 0.0 copy-start.1
  0.7 0.0 copy-start.2
  0.7 0.0 copy-start.3
  0.7 0.0 copy-start.4
  0.7 0.0 copy-start.5
  0.7 10.7 %front.1 = (bf16[3840,128]{1,0:T(8,128)(2,1)}, s32[4,16,128]{2,1,0:T(8,128)S(1)}, f32[1,1]{1,0:T(1,128)}) custom-call(bf16[137,8461]{1,0:T(8,128)(2,1)} %bitcast.12, s32[1,96]{1,0:T(1,128)} %bitcast.21, bf16[137,40,128]{2,1,0:T(8,128)(2,1)} %bitcast.13, s32[16,32]{1,0:T(8,128)} %bitcast.20), custom_call_target="tpu_custom_call" | custom-call | tf_op jit(solution)/shard_map/front/pallas_call | solution.py:818
  12.0 0.0 copy-done
  12.0 0.0 copy-done.1
  12.0 0.0 copy-done.2
  12.0 0.0 copy-done.3
  12.0 0.0 copy-done.4
  12.0 0.0 copy-done.5
  12.0 63.9 %conditional.1 = ((f32[96,40,512]{2,1,0:T(8,128)}, bf16[137,40,128]{2,1,0:T(8,128)(2,1)})) conditional(s32[]{:T(128)} %bitcast.4, (bf16[3840,128]{1,0:T(8,128)(2,1)}, s32[4,16,128]{2,1,0:T(8,128)S(1)}, bf16[137,40,128]{2,1,0:T(8,128)(2,1)S(1)}, bf16[80,80]{1,0:T(8,128)(2,1)S(1)}, bf16[137,128]{1,0:T(8,128)(2,1)S(1)}, ...), branch_computations={%region_0.0_spmd, %region_1.0_spmd} | conditional | bytes 8 | solution.py:930
  12.1 56.8 %exchange_tight.1 = (bf16[16,960,128]{2,1,0:T(8,128)(2,1)S(1)}, bf16[137,40,128]{2,1,0:T(8,128)(2,1)S(1)}, bf16[512,512]{1,0:T(8,128)(2,1)S(1)}) custom-call(bf16[3840,128]{1,0:T(8,128)(2,1)} %get-tuple-element.44.owned_ref, s32[4,16,128]{2,1,0:T(8,128)S(1)} %get-tuple-element.45.tables_ref, bf16[137,40,128]{2,1,0:T(8,128)(2,1)S(1)} %get-tuple-element.46.anom_ref, ...), custom_call_target="tpu_custom_call" | custom-call | tf_op jit(solution)/shard_map/cond/branch_1_fun/exchange_tight/pallas_call | solution.py:864
  68.9 7.0 %combine.3 = (f32[96,40,512]{2,1,0:T(8,128)}, bf16[137,40,128]{2,1,0:T(8,128)(2,1)}) custom-call(f32[96]{0:T(128)S(1)} %get-tuple-element.43.bias_ref, bf16[16,960,128]{2,1,0:T(8,128)(2,1)S(1)} %get-tuple-element.51.recv_ref, bf16[512,512]{1,0:T(8,128)(2,1)S(1)} %get-tuple-element.52.spread_ref, bf16[137,40,128]{2,1,0:T(8,128)(2,1)S(1)} %get-tuple-element.53.mixed_ref), custom_call_target="tpu_custom_call" | custom-call | tf_op jit(solution)/shard_map/cond/branch_1_fun/combine/pallas_call | solution.py:897
Async XLA Ops:
  0.6 11.4 %copy-start = (bf16[40,137,128]{2,0,1:T(8,128)(2,1)S(1)}, bf16[40,137,128]{2,0,1:T(8,128)(2,1)}, u32[]{:S(2)}) copy-start(bf16[40,137,128]{2,0,1:T(8,128)(2,1)} %param.12) | copy-start | bytes 4208644
  0.6 11.4 %copy-start.1 = (bf16[137,128]{1,0:T(8,128)(2,1)S(1)}, bf16[137,128]{1,0:T(8,128)(2,1)}, u32[]{:S(2)}) copy-start(bf16[137,128]{1,0:T(8,128)(2,1)} %param.14) | copy-start | bytes 105220
  0.7 11.4 %copy-start.2 = (bf16[1,80,80]{2,1,0:T(8,128)(2,1)S(1)}, bf16[1,80,80]{2,1,0:T(8,128)(2,1)}, u32[]{:S(2)}) copy-start(bf16[1,80,80]{2,1,0:T(8,128)(2,1)} %param.13) | copy-start | bytes 38404
  0.7 11.4 %copy-start.3 = (s32[512,4]{0,1:T(4,128)S(1)}, s32[512,4]{0,1:T(4,128)}, u32[]{:S(2)}) copy-start(s32[512,4]{0,1:T(4,128)} %param.19) | copy-start | bytes 24580
  0.7 11.4 %copy-start.4 = (bf16[512,4]{0,1:T(4,128)(2,1)S(1)}, bf16[512,4]{0,1:T(4,128)(2,1)}, u32[]{:S(2)}) copy-start(bf16[512,4]{0,1:T(4,128)(2,1)} %param.20) | copy-start | bytes 12292
  0.7 11.4 %copy-start.5 = (f32[96]{0:T(128)S(1)}, f32[96]{0:T(128)}, u32[]{:S(2)}) copy-start(f32[96]{0:T(128)} %param.21) | copy-start | bytes 1156

commit v4 on v3

--- a/solution.py
+++ b/solution.py
@@ -15,6 +15,7 @@
 OWN, OUTER, PARTNER, FAR = range(4)
 AWAY = {OWN: 0, PARTNER: 1, FAR: 2}
 CAP = 80
+WIDE = 112
 FOLD = 8
 
 
@@ -78,7 +79,9 @@
     for far in (0, ZONES - 1):
         mask = needed(message, 0, far * zone_tiles, zone_tiles, cols)
         total = jnp.sum(mask, axis=0, keepdims=True)
-        most = jnp.maximum(most, jnp.where(zone == far, 0.0, total))
+        most = jnp.maximum(most, jnp.where(zone == far, 0.0, total - CAP))
+    across = needed(message, 0, (1 - zone // 2) * (n // 2), n // 2, cols)
+    most = jnp.maximum(most, jnp.sum(across, axis=0, keepdims=True) - WIDE)
     counted[0] = jnp.broadcast_to(most, (1, LANES)).astype(jnp.int32)
     pl.semaphore_wait(barrier, n - 1)
 
@@ -184,6 +187,10 @@
     picks,
     away_picks,
     open_picks,
+    cross_buf,
+    cross_in,
+    cross_picks,
+    narrow_picks,
     pieces,
     mixed,
     spread,
@@ -197,6 +204,8 @@
     p_send,
     away_send,
     away_recv,
+    cross_send,
+    cross_recv,
     a_recv,
     local_sem,
 ):
@@ -282,43 +291,70 @@
     def build_near(block):
         build(source[block], zone_base, picks, block)
 
+    half = n // 2
+    half_base = (zone // 2) * half
+    other_base = half - half_base
+
+    def fold_columns(mask, cap, g):
+        place_of = positions(mask, cols)[:, 0:1].astype(jnp.int32) + g * cap
+        place_of = jnp.where(mask > 0.0, place_of, -1)
+        lane = lax.broadcasted_iota(jnp.int32, (cols, FOLD * cap), 1)
+        return jnp.where(lane == place_of, 1.0, 0.0).astype(jnp.bfloat16)
+
+    def build_fold(into, origin, base, count, cap):
+        mask = needed(tables_ref, origin // zone_tiles, base, count, cols)
+        for g in range(FOLD):
+            into[g * cols : (g + 1) * cols, :] = fold_columns(mask, cap, g)
+
     def build_away(block):
-        origin = source[block]
-        if not tight:
-            build(origin, away_base, away_picks, AWAY[block])
-            return
-        mask = needed(tables_ref, origin // zone_tiles, away_base, zone_tiles, cols)
-        place_of = positions(mask, cols)[:, 0:1].astype(jnp.int32)
-        place_of = jnp.where(mask > 0.0, place_of, -FOLD * CAP)
-        lane = lax.broadcasted_iota(jnp.int32, (cols, FOLD * CAP), 1)
+        if tight:
+            build_fold(away_picks.at[AWAY[block]], source[block], away_base, zone_tiles, CAP)
+        else:
+            build(source[block], away_base, away_picks, AWAY[block])
+
+    def build_cross(i):
+        build_fold(cross_picks.at[i], source[i], other_base, half, WIDE)
+
+    def build_narrow(block):
+        line = source[block] // zone_tiles
+        wide_mask = needed(tables_ref, line, half_base, half, cols)
+        wide_place = jnp.where(wide_mask > 0.0, positions(wide_mask, cols), -1.0)
+        wide_place = jnp.transpose(wide_place)[0:1, :].astype(jnp.int32)
+        row_id = lax.broadcasted_iota(jnp.int32, (WIDE, cols), 0)
+        back = jnp.where(row_id == wide_place, 1.0, 0.0).astype(jnp.bfloat16)
+        mask = needed(tables_ref, line, away_base, zone_tiles, cols)
         for g in range(FOLD):
-            away_picks[AWAY[block], g * cols : (g + 1) * cols, :] = jnp.where(
-                lane == place_of + g * CAP, 1.0, 0.0
+            narrow_picks[block - PARTNER, g * WIDE : (g + 1) * WIDE, :] = jnp.dot(
+                back, fold_columns(mask, CAP, g), preferred_element_type=jnp.float32
             ).astype(jnp.bfloat16)
 
-    def build_open(i):
-        origin = source[1 + i]
-        mask = needed(tables_ref, origin // zone_tiles, zone_base, zone_tiles, cols)
+    def build_open(i, origin, base, count, cap):
+        line = origin // zone_tiles
+        mask = needed(tables_ref, line, base, count, cols)
         column = lax.broadcasted_iota(jnp.int32, (cols, LANES), 0)
-        row_id = lax.broadcasted_iota(jnp.int32, (FOLD * CAP, 2 * LANES), 0)
+        row_id = lax.broadcasted_iota(jnp.int32, (FOLD * cap, 2 * LANES), 0)
 
         def one(t, carry):
-            row = tables_ref[origin // zone_tiles, pl.ds(zone_base + t, 1), :]
+            row = tables_ref[line, pl.ds(zone_base + t, 1), :]
             ahead_of = jnp.where(column < row, mask, 0.0)
             spot = jnp.sum(ahead_of, axis=0, keepdims=True).astype(jnp.int32)
             wants = jnp.concatenate(
-                [spot + (2 * lane_group + v) * CAP for v in range(2)], axis=1
+                [spot + (2 * lane_group + v) * cap for v in range(2)], axis=1
             )
-            open_picks[i, t] = jnp.where(row_id == wants, 1.0, 0.0).astype(jnp.bfloat16)
+            open_picks[i, t, 0 : FOLD * cap] = jnp.where(row_id == wants, 1.0, 0.0).astype(
+                jnp.bfloat16
+            )
             return carry
 
         lax.fori_loop(0, zone_tiles, one, 0)
-
-    build_near(OWN)
 
     @pl.when(inner)
     def _():
+        if tight:
+            build_cross(OWN)
         build_away(OWN)
+
+    build_near(OWN)
 
     greeted = zone_tiles - 1 + nm - 1 + jnp.where(inner, 2, 1) * zone_tiles
     pl.semaphore_wait(barrier, greeted)
@@ -329,7 +365,7 @@
     def narrow(c):
         return pl.ds(pl.multiple_of(c * part, part), part)
 
-    landing = jnp.where(inner, 1, 0)
+    landing = 0 if tight else jnp.where(inner, 1, 0)
 
     def own_stream(c):
         return pltpu.make_async_remote_copy(
@@ -407,6 +443,16 @@
             device_id_type=MESH,
         )
 
+    def cross(i, c):
+        return pltpu.make_async_remote_copy(
+            src_ref=cross_buf.at[i, folded(c)],
+            dst_ref=cross_in.at[i, folded(c)],
+            send_sem=cross_send.at[i],
+            recv_sem=cross_recv.at[i, c],
+            device_id=(ahead, mem),
+            device_id_type=MESH,
+        )
+
     def spread_out_rows(block, c, count, size):
         block_ref = owned_ref if block == OWN else block_buf.at[block - 1]
         return jnp.concatenate(
@@ -432,19 +478,28 @@
     def pack_near(block, c):
         pack(block, c, picks, block, send_buf)
 
+    def pack_cross(i, c):
+        wide = spread_out_rows(i, c, FOLD, fold_part)
+        out = jnp.dot(wide, cross_picks[i], preferred_element_type=jnp.float32)
+        cross_buf[i, folded(c)] = out.astype(jnp.bfloat16)
+
     def pack_away(block, c):
         if not tight:
             pack(block, c, away_picks, AWAY[block], away_buf)
             return
-        wide = spread_out_rows(block, c, FOLD, fold_part)
-        out = jnp.dot(wide, away_picks[AWAY[block]], preferred_element_type=jnp.float32)
+        if block == OWN:
+            wide, pick = spread_out_rows(OWN, c, FOLD, fold_part), away_picks[AWAY[OWN]]
+        else:
+            i = block - PARTNER
+            wide, pick = cross_in[i, folded(c)], narrow_picks[i]
+        out = jnp.dot(wide, pick, preferred_element_type=jnp.float32)
         away_buf[AWAY[block], folded(c)] = out.astype(jnp.bfloat16)
 
-    def unpack(i, c):
-        held = compact_buf[i, folded(c)]
-
+    def unpack(held, i, cap, c):
         def one(t, carry):
-            out = jnp.dot(held, open_picks[i, t], preferred_element_type=jnp.float32)
+            out = jnp.dot(
+                held, open_picks[i, t, 0 : FOLD * cap], preferred_element_type=jnp.float32
+            )
             out = out.astype(jnp.bfloat16)
             for v in range(2):
                 rows_of = pl.ds(
@@ -485,19 +540,30 @@
         own_stream(c).start()
         return carry
 
-    lax.fori_loop(0, chunks, start_own, 0)
+    if tight:
+
+        @pl.when(outer)
+        def _():
+            lax.fori_loop(0, chunks, start_own, 0)
+    else:
+        lax.fori_loop(0, chunks, start_own, 0)
+
+    def later(block, c):
+        @pl.when(c > 0)
+        def _():
+            send_near(block, c - 1)
 
     @pl.when(inner)
     def _():
         def own_step(c, carry):
+            if tight:
+                pack_cross(OWN, c)
             pack_away(OWN, c)
+            if tight:
+                cross(OWN, c).start()
             pack_near(OWN, c)
             send_away(OWN, c)
-
-            @pl.when(c > 0)
-            def _():
-                send_near(OWN, c - 1)
-
+            later(OWN, c)
             return carry
 
         lax.fori_loop(0, chunks, own_step, 0)
@@ -506,11 +572,7 @@
     def _():
         def own_step(c, carry):
             pack_near(OWN, c)
-
-            @pl.when(c > 0)
-            def _():
-                send_near(OWN, c - 1)
-
+            later(OWN, c)
             return carry
 
         lax.fori_loop(0, chunks, own_step, 0)
@@ -520,8 +582,13 @@
 
     @pl.when(inner)
     def _():
-        build_away(PARTNER)
-        build_near(PARTNER)
+        if tight:
+            build_cross(OUTER)
+            build_narrow(PARTNER)
+            build_open(PARTNER - 1, source[PARTNER], half_base, half, WIDE)
+        else:
+            build_away(PARTNER)
+            build_near(PARTNER)
         build_near(OUTER)
 
     send_near(OWN, chunks - 1)
@@ -531,37 +598,45 @@
     def _():
         def mid_step(c, carry):
             stream_arrival(OUTER, c).wait_recv()
-            forward_stream(c).start()
-            stream_arrival(PARTNER, c).wait_recv()
-            pack_away(PARTNER, c)
-            pack_near(PARTNER, c)
+            if tight:
+                pack_cross(OUTER, c)
+                cross(PARTNER - PARTNER, c).wait_recv()
+                pack_away(PARTNER, c)
+                cross(OUTER, c).start()
+                unpack(cross_in[0, folded(c)], PARTNER - 1, WIDE, c)
+            else:
+                forward_stream(c).start()
+                stream_arrival(PARTNER, c).wait_recv()
+                pack_away(PARTNER, c)
+                pack_near(PARTNER, c)
             send_away(PARTNER, c)
             pack_near(OUTER, c)
             send_near(PARTNER, c)
-
-            @pl.when(c > 0)
-            def _():
-                send_near(OUTER, c - 1)
-
+            later(OUTER, c)
             return carry
 
         lax.fori_loop(0, chunks, mid_step, 0)
-        build_away(FAR)
-        build_near(FAR)
+        if tight:
+            build_narrow(FAR)
+            build_open(FAR - 1, source[FAR], half_base, half, WIDE)
+        else:
+            build_away(FAR)
+            build_near(FAR)
         send_near(OUTER, chunks - 1)
         keep(OUTER).start()
         keep(PARTNER).start()
 
         def far_step(c, carry):
-            stream_arrival(FAR, c).wait_recv()
-            pack_away(FAR, c)
-            pack_near(FAR, c)
+            if tight:
+                cross(FAR - PARTNER, c).wait_recv()
+                pack_away(FAR, c)
+                unpack(cross_in[1, folded(c)], FAR - 1, WIDE, c)
+            else:
+                stream_arrival(FAR, c).wait_recv()
+                pack_away(FAR, c)
+                pack_near(FAR, c)
             send_away(FAR, c)
-
-            @pl.when(c > 0)
-            def _():
-                send_near(FAR, c - 1)
-
+            later(FAR, c)
             return carry
 
         lax.fori_loop(0, chunks, far_step, 0)
@@ -583,7 +658,7 @@
         @pl.when(outer)
         def _():
             for i in range(3):
-                build_open(i)
+                build_open(i, source[1 + i], zone_base, zone_tiles, CAP)
 
     lax.fori_loop(0, n, spread_rows, 0)
 
@@ -597,7 +672,7 @@
         def open_compact(i):
             def step(c, carry):
                 compact(i, c).wait_recv()
-                unpack(i, c)
+                unpack(compact_buf[i, folded(c)], i, CAP, c)
 
                 @pl.when(c > 0)
                 def _():
@@ -685,7 +760,8 @@
             device_id_type=MESH,
         ).wait_recv()
 
-    gone(owned_ref, stream_send.at[0])
+    if not tight:
+        gone(owned_ref, stream_send.at[0])
     gone(send_buf.at[OWN, pl.ds(0, zone_tiles - 1)], p_send.at[OWN])
 
     def line_sent():
@@ -695,7 +771,11 @@
 
     @pl.when(inner)
     def _():
-        gone(block_buf.at[0], stream_send.at[1])
+        if tight:
+            for i in (OWN, OUTER):
+                gone(cross_buf.at[i], cross_send.at[i])
+        else:
+            gone(block_buf.at[0], stream_send.at[1])
         for block in AWAY:
             gone(away_buf.at[AWAY[block]], away_send.at[AWAY[block]])
         line_sent()
@@ -703,6 +783,7 @@
     @pl.when(outer)
     def _():
         if tight:
+            gone(owned_ref, stream_send.at[0])
             line_sent()
             come(n - ZONES)
         else:
@@ -718,34 +799,39 @@
 
 
 def combine_kernel(
-    n, groups, bias_ref, recv_ref, spread_ref, mixed_ref, out_ref, analysis_ref, sem
+    n, steps, bias_ref, recv_ref, spread_ref, mixed_ref, out_ref, analysis_ref, prior, sems
 ):
-    step = pl.program_id(0)
-    carry_out = pltpu.make_async_copy(mixed_ref, analysis_ref, sem)
-
-    @pl.when(step == 0)
-    def _():
-        carry_out.start()
-
+    carry_out = pltpu.make_async_copy(mixed_ref, analysis_ref, sems.at[steps])
     slots = spread_ref.shape[0] // n
-    channels, members = out_ref.shape[0], out_ref.shape[1]
-    stacked = jnp.concatenate(
-        [
-            jnp.concatenate(
-                [recv_ref[s, :, g * slots : (g + 1) * slots] for s in range(n)], axis=1
-            )
-            for g in range(groups)
-        ],
-        axis=0,
-    )
-    prior = jnp.dot(stacked, spread_ref[...], preferred_element_type=jnp.float32)
-    for c in range(channels):
-        bias = bias_ref[step * channels + c]
-        out_ref[c] = prior[c * members : (c + 1) * members, :] + bias
-
-    @pl.when(step == pl.num_programs(0) - 1)
-    def _():
-        carry_out.wait()
+    groups = LANES // slots
+    members = prior.shape[1]
+    channels = prior.shape[0] // steps
+    part = recv_ref.shape[1] // steps
+
+    def move(step):
+        span = pl.ds(step * channels, channels)
+        return pltpu.make_async_copy(prior.at[span], out_ref.at[span], sems.at[step])
+
+    for step in range(steps):
+        rows_of = slice(step * part, (step + 1) * part)
+        stacked = jnp.concatenate(
+            [
+                jnp.concatenate(
+                    [recv_ref[s, rows_of, g * slots : (g + 1) * slots] for s in range(n)], axis=1
+                )
+                for g in range(groups)
+            ],
+            axis=0,
+        )
+        total = jnp.dot(stacked, spread_ref[...], preferred_element_type=jnp.float32)
+        for c in range(channels):
+            bias = bias_ref[step * channels + c]
+            prior[step * channels + c] = total[c * members : (c + 1) * members, :] + bias
+        move(step).start()
+    carry_out.start()
+    for step in range(steps):
+        move(step).wait()
+    carry_out.wait()
 
 
 def chunk_count(channels, mem_dev, groups):
@@ -842,25 +928,31 @@
 
     def rest(tight, owned, tables, anomalies, weights, mean, footprint, footprint_weight, bias):
         part = rows // groups
+        pairs = zone_tiles // 2
+        spare = (8, LANES)
+        fold_rows, capped, widened = rows // FOLD, FOLD * CAP, FOLD * WIDE
         if tight:
             variant = [
-                pltpu.VMEM((3, rows // FOLD, FOLD * CAP), jnp.bfloat16),
-                pltpu.VMEM((3, rows, cols), jnp.bfloat16),
-                pltpu.VMEM((3, rows // FOLD, FOLD * CAP), jnp.bfloat16),
-                pltpu.VMEM((4, zone_tiles // 2, groups * cols, 2 * LANES), jnp.bfloat16),
-                pltpu.VMEM((3, FOLD * cols, FOLD * CAP), jnp.bfloat16),
-                pltpu.VMEM((3, zone_tiles, FOLD * CAP, 2 * LANES), jnp.bfloat16),
+                (3, fold_rows, capped),
+                (1, rows, cols),
+                (3, fold_rows, capped),
+                (2, pairs, groups * cols, 2 * LANES),
+                (1, FOLD * cols, capped),
+                (3, zone_tiles, widened, 2 * LANES),
+                (2, fold_rows, widened),
+                (2, fold_rows, widened),
+                (2, FOLD * cols, widened),
+                (2, widened, capped),
             ]
         else:
-            spare = pltpu.VMEM((8, LANES), jnp.bfloat16)
             variant = [
-                pltpu.VMEM((3, zone_tiles, part, LANES), jnp.bfloat16),
-                pltpu.VMEM((3, rows, cols), jnp.bfloat16),
+                (3, zone_tiles, part, LANES),
+                (3, rows, cols),
                 spare,
-                pltpu.VMEM((4, zone_tiles // 2, groups * cols, 2 * LANES), jnp.bfloat16),
-                pltpu.VMEM((3, zone_tiles // 2, groups * cols, 2 * LANES), jnp.bfloat16),
-                spare,
-            ]
+                (4, pairs, groups * cols, 2 * LANES),
+                (3, pairs, groups * cols, 2 * LANES),
+            ] + [spare] * 5
+        variant = [pltpu.VMEM(shape, jnp.bfloat16) for shape in variant]
         received, mixed, spread = pl.pallas_call(
             functools.partial(exchange_kernel, n, nm, chunks, tight),
             out_shape=(
@@ -886,6 +978,8 @@
                 dma((4,)),
                 dma((3,)),
                 dma((3, chunks)),
+                dma((2,)),
+                dma((2, chunks)),
                 dma((1,)),
                 dma((8,)),
             ],
@@ -895,24 +989,18 @@
             name="exchange_tight" if tight else "exchange",
         )(owned, tables, anomalies, weights, mean, footprint, footprint_weight)
         return pl.pallas_call(
-            functools.partial(combine_kernel, n, groups),
+            functools.partial(combine_kernel, n, chunks),
             out_shape=(
                 jax.ShapeDtypeStruct((channels, mem_dev, obs), jnp.float32),
                 jax.ShapeDtypeStruct(mixed.shape, mixed.dtype),
             ),
-            grid=(chunks,),
-            in_specs=[
-                pl.BlockSpec(memory_space=pltpu.SMEM),
-                pl.BlockSpec((n, part // chunks, LANES), lambda i: (0, i, 0)),
-                pl.BlockSpec((n * slots, obs), lambda i: (0, 0)),
-                vmem,
+            in_specs=[pl.BlockSpec(memory_space=pltpu.SMEM), vmem, vmem, vmem],
+            out_specs=(hbm, hbm),
+            scratch_shapes=[
+                pltpu.VMEM((channels, mem_dev, obs), jnp.float32),
+                dma((chunks + 1,)),
             ],
-            out_specs=(
-                pl.BlockSpec((channels // chunks, mem_dev, obs), lambda i: (i, 0, 0)),
-                hbm,
-            ),
-            scratch_shapes=[dma],
-            compiler_params=pltpu.CompilerParams(vmem_limit_bytes=24 * 1024 * 1024),
+            compiler_params=pltpu.CompilerParams(vmem_limit_bytes=40 * 1024 * 1024),
             name="combine",
         )(bias, received, spread, mixed)
 
@@ -928,7 +1016,7 @@
     )
     if foldable:
         prior, analysis = lax.cond(
-            count[0, 0] <= CAP,
+            count[0, 0] <= 0,
             functools.partial(rest, True),
             functools.partial(rest, False),
             *operands,

time: 76.2 us -> 72.2 us (0.948)
  Pallas kernels: 74.5 us -> 70.2 us
    pallas_call x1, Pallas kernels: 56.8 us -> 53.8 us  [rest(): pl.pallas_call(functools.partial(exchange_kernel, n, nm, chunks, tight),...]
    pallas_call x1, Pallas kernels: 7.02 us -> 5.73 us  [rest(): pl.pallas_call(functools.partial(combine_kernel, n, chunks), out_shape=(j...]
where the time goes in v4:
time: 72.2 us; the launch traced here: 72 us
  Pallas kernels  70.2 us (97%)
  between operations  1.54 us (2%)
    pallas_call x1, Pallas kernels, rest(): pl.pallas_call(functools.partial(exchange_kernel, n, nm, chunks, tight),...  53.8 us
    pallas_call x1, Pallas kernels, shards(): pl.pallas_call(functools.partial(front_kernel, n, select), out_shape=tupl...  10.6 us
    pallas_call x1, Pallas kernels, rest(): pl.pallas_call(functools.partial(combine_kernel, n, chunks), out_shape=(j...  5.73 us

profile of v4, /device:TPU:0, one launch (start us, length us, event | category | flops | bytes accessed | tf_op | source)
XLA Modules:
  0.0 72.0 jit_solution(8168818574899845319)
XLA Ops:
  0.6 0.0 copy-start
  0.6 0.0 copy-start.1
  0.7 0.0 copy-start.2
  0.7 0.0 copy-start.3
  0.7 0.0 copy-start.4
  0.7 0.0 copy-start.5
  0.7 10.6 %front.1 = (bf16[3840,128]{1,0:T(8,128)(2,1)}, s32[4,16,128]{2,1,0:T(8,128)S(1)}, f32[1,1]{1,0:T(1,128)}) custom-call(bf16[137,8461]{1,0:T(8,128)(2,1)} %bitcast.12, s32[1,96]{1,0:T(1,128)} %bitcast.21, bf16[137,40,128]{2,1,0:T(8,128)(2,1)} %bitcast.13, s32[16,32]{1,0:T(8,128)} %bitcast.20), custom_call_target="tpu_custom_call" | custom-call | tf_op jit(solution)/shard_map/front/pallas_call | solution.py:904
  12.0 0.0 copy-done
  12.0 0.0 copy-done.1
  12.0 0.0 copy-done.2
  12.0 0.0 copy-done.3
  12.0 0.0 copy-done.4
  12.0 0.0 copy-done.5
  12.0 59.8 %conditional.1 = ((f32[96,40,512]{2,1,0:T(8,128)}, bf16[137,40,128]{2,1,0:T(8,128)(2,1)})) conditional(s32[]{:T(128)} %bitcast.4, (bf16[3840,128]{1,0:T(8,128)(2,1)}, s32[4,16,128]{2,1,0:T(8,128)S(1)}, bf16[137,40,128]{2,1,0:T(8,128)(2,1)S(1)}, bf16[80,80]{1,0:T(8,128)(2,1)S(1)}, bf16[137,128]{1,0:T(8,128)(2,1)S(1)}, ...), branch_computations={%region_0.0_spmd, %region_1.0_spmd} | conditional | bytes 8 | solution.py:1018
  12.0 53.8 %exchange_tight.1 = (bf16[16,960,128]{2,1,0:T(8,128)(2,1)S(1)}, bf16[137,40,128]{2,1,0:T(8,128)(2,1)S(1)}, bf16[512,512]{1,0:T(8,128)(2,1)S(1)}) custom-call(bf16[3840,128]{1,0:T(8,128)(2,1)} %get-tuple-element.44.owned_ref, s32[4,16,128]{2,1,0:T(8,128)S(1)} %get-tuple-element.45.tables_ref, bf16[137,40,128]{2,1,0:T(8,128)(2,1)S(1)} %get-tuple-element.46.anom_ref, ...), custom_call_target="tpu_custom_call" | custom-call | tf_op jit(solution)/shard_map/cond/branch_1_fun/exchange_tight/pallas_call | solution.py:956
  65.8 5.7 %combine.3 = (f32[96,40,512]{2,1,0:T(8,128)}, bf16[137,40,128]{2,1,0:T(8,128)(2,1)}) custom-call(f32[96]{0:T(128)S(1)} %get-tuple-element.43.bias_ref, bf16[16,960,128]{2,1,0:T(8,128)(2,1)S(1)} %get-tuple-element.51.recv_ref, bf16[512,512]{1,0:T(8,128)(2,1)S(1)} %get-tuple-element.52.spread_ref, bf16[137,40,128]{2,1,0:T(8,128)(2,1)S(1)} %get-tuple-element.53.mixed_ref), custom_call_target="tpu_custom_call" | custom-call | tf_op jit(solution)/shard_map/cond/branch_1_fun/combine/pallas_call | solution.py:991
Async XLA Ops:
  0.6 11.3 %copy-start = (bf16[40,137,128]{2,0,1:T(8,128)(2,1)S(1)}, bf16[40,137,128]{2,0,1:T(8,128)(2,1)}, u32[]{:S(2)}) copy-start(bf16[40,137,128]{2,0,1:T(8,128)(2,1)} %param.12) | copy-start | bytes 4208644
  0.6 11.3 %copy-start.1 = (bf16[137,128]{1,0:T(8,128)(2,1)S(1)}, bf16[137,128]{1,0:T(8,128)(2,1)}, u32[]{:S(2)}) copy-start(bf16[137,128]{1,0:T(8,128)(2,1)} %param.14) | copy-start | bytes 105220
  0.7 11.3 %copy-start.2 = (bf16[1,80,80]{2,1,0:T(8,128)(2,1)S(1)}, bf16[1,80,80]{2,1,0:T(8,128)(2,1)}, u32[]{:S(2)}) copy-start(bf16[1,80,80]{2,1,0:T(8,128)(2,1)} %param.13) | copy-start | bytes 38404
  0.7 11.3 %copy-start.3 = (s32[512,4]{0,1:T(4,128)S(1)}, s32[512,4]{0,1:T(4,128)}, u32[]{:S(2)}) copy-start(s32[512,4]{0,1:T(4,128)} %param.19) | copy-start | bytes 24580
  0.7 11.3 %copy-start.4 = (bf16[512,4]{0,1:T(4,128)(2,1)S(1)}, bf16[512,4]{0,1:T(4,128)(2,1)}, u32[]{:S(2)}) copy-start(bf16[512,4]{0,1:T(4,128)(2,1)} %param.20) | copy-start | bytes 12292
  0.7 11.3 %copy-start.5 = (f32[96]{0:T(128)S(1)}, f32[96]{0:T(128)}, u32[]{:S(2)}) copy-start(f32[96]{0:T(128)} %param.21) | copy-start | bytes 1156

commit v5 on v4

--- a/solution.py
+++ b/solution.py
@@ -536,6 +536,9 @@
             send_buf.at[block, place], recv_ref.at[source[block]], local_sem.at[4 + block]
         )
 
+    for k in range(1, nm):
+        member_copy(k).start()
+
     def start_own(c, carry):
         own_stream(c).start()
         return carry
@@ -576,9 +579,6 @@
             return carry
 
         lax.fori_loop(0, chunks, own_step, 0)
-
-    for k in range(1, nm):
-        member_copy(k).start()
 
     @pl.when(inner)
     def _():
@@ -667,47 +667,24 @@
         send_near(FAR, chunks - 1)
         keep(FAR).start()
 
-    if tight:
-
-        def open_compact(i):
-            def step(c, carry):
-                compact(i, c).wait_recv()
-                unpack(compact_buf[i, folded(c)], i, CAP, c)
-
-                @pl.when(c > 0)
-                def _():
-                    send_near(1 + i, c - 1)
-
-                return carry
-
-            lax.fori_loop(0, chunks, step, 0)
-
-        @pl.when(outer)
-        def _():
-            open_compact(0)
-            send_near(1, chunks - 1)
-            keep(1).start()
-            open_compact(1)
-            send_near(2, chunks - 1)
-            keep(2).start()
-
     spread_out = pltpu.make_async_copy(spread, spread_ref, local_sem.at[2])
     spread_out.start()
-    for k in range(1, nm):
-        pltpu.make_async_remote_copy(
-            src_ref=anom_ref,
-            dst_ref=pieces.at[k - 1],
-            send_sem=m_send.at[k],
-            recv_sem=m_recv.at[k],
-            device_id=(tile, lax.rem(mem + k, nm)),
-            device_id_type=MESH,
-        ).wait()
-
     mean_wide[...] = mean_ref[...].astype(jnp.float32)
     weight_wide[...] = jnp.transpose(weight_ref[...].astype(jnp.float32))
     mine = weight_wide[pl.ds(mem * mem_dev, mem_dev), :].astype(jnp.bfloat16)
     for p in range(nm):
         shares[p] = mine[:, p * mem_dev : (p + 1) * mem_dev]
+
+    def members_here():
+        for k in range(1, nm):
+            pltpu.make_async_remote_copy(
+                src_ref=anom_ref,
+                dst_ref=pieces.at[k - 1],
+                send_sem=m_send.at[k],
+                recv_sem=m_recv.at[k],
+                device_id=(tile, lax.rem(mem + k, nm)),
+                device_id_type=MESH,
+            ).wait()
 
     def mix(first, count):
         mixture = jnp.zeros((mem_dev, count * cols), jnp.float32)
@@ -725,20 +702,51 @@
         return carry
 
     full = levels // MIX_LEVELS
-    lax.fori_loop(0, full, mix_block, 0)
+    per = -(-full // chunks)
+
+    def mix_share(c):
+        lax.fori_loop(c * per, jnp.minimum((c + 1) * per, full), mix_block, 0)
+
+    def mix_step(c, carry):
+        mix_share(c)
+        return carry
+
+    if tight:
+
+        def open_compact(i, mixing):
+            def step(c, carry):
+                compact(i, c).wait_recv()
+                unpack(compact_buf[i, folded(c)], i, CAP, c)
+                later(1 + i, c)
+                if mixing:
+                    mix_share(c)
+                return carry
+
+            lax.fori_loop(0, chunks, step, 0)
+            send_near(1 + i, chunks - 1)
+            keep(1 + i).start()
+
+        @pl.when(outer)
+        def _():
+            open_compact(0, False)
+            open_compact(1, False)
+            members_here()
+            open_compact(2, True)
+
+        @pl.when(inner)
+        def _():
+            members_here()
+            lax.fori_loop(0, chunks, mix_step, 0)
+
+    else:
+        members_here()
+        lax.fori_loop(0, chunks, mix_step, 0)
+
     if levels % MIX_LEVELS:
         mix(full * MIX_LEVELS, levels % MIX_LEVELS)
 
     analysis_out = pltpu.make_async_copy(mixed, analysis_ref, local_sem.at[3])
     analysis_out.start()
-
-    if tight:
-
-        @pl.when(outer)
-        def _():
-            open_compact(2)
-            send_near(3, chunks - 1)
-            keep(3).start()
 
     def gone(ref, sem):
         pltpu.make_async_remote_copy(
@@ -812,6 +820,7 @@
         span = pl.ds(step * channels, channels)
         return pltpu.make_async_copy(prior.at[span], out_ref.at[span], sems.at[step])
 
+    carry_out.start()
     for step in range(steps):
         rows_of = slice(step * part, (step + 1) * part)
         stacked = jnp.concatenate(
@@ -828,7 +837,6 @@
             bias = bias_ref[step * channels + c]
             prior[step * channels + c] = total[c * members : (c + 1) * members, :] + bias
         move(step).start()
-    carry_out.start()
     for step in range(steps):
         move(step).wait()
     carry_out.wait()
@@ -908,7 +916,7 @@
         out_specs=(vmem,) * (len(front_out) - 1) + (pl.BlockSpec(memory_space=pltpu.SMEM),),
         scratch_shapes=front_scratch + [dma((2,)), dma((2,)), dma((2,))],
         compiler_params=pltpu.CompilerParams(
-            collective_id=0, has_side_effects=True, vmem_limit_bytes=62 * 1024 * 1024
+            collective_id=0, has_side_effects=True, vmem_limit_bytes=58 * 1024 * 1024
         ),
         name="front",
     )(*front_args)

time: 72.2 us -> 69.1 us (0.957)
  Pallas kernels: 70.2 us -> 67.1 us
    pallas_call x1, Pallas kernels: 53.8 us -> 51.6 us  [rest(): pl.pallas_call(functools.partial(exchange_kernel, n, nm, chunks, tight),...]
where the time goes in v5:
time: 69.1 us; the launch traced here: 68.9 us
  Pallas kernels  67.1 us (97%)
  between operations  1.55 us (2%)
    pallas_call x1, Pallas kernels, rest(): pl.pallas_call(functools.partial(exchange_kernel, n, nm, chunks, tight),...  51.6 us
    pallas_call x1, Pallas kernels, shards(): pl.pallas_call(functools.partial(front_kernel, n, select), out_shape=tupl...  10.2 us
    pallas_call x1, Pallas kernels, rest(): pl.pallas_call(functools.partial(combine_kernel, n, chunks), out_shape=(j...  5.32 us

profile of v5, /device:TPU:0, one launch (start us, length us, event | category | flops | bytes accessed | tf_op | source)
XLA Modules:
  0.0 68.9 jit_solution(5442016062257043681)
XLA Ops:
  0.6 0.0 copy-start
  0.6 0.0 copy-start.1
  0.7 0.0 copy-start.2
  0.7 0.0 copy-start.3
  0.7 0.0 copy-start.4
  0.7 0.0 copy-start.5
  0.7 10.2 %front.1 = (bf16[3840,128]{1,0:T(8,128)(2,1)S(1)}, s32[4,16,128]{2,1,0:T(8,128)S(1)}, f32[1,1]{1,0:T(1,128)}) custom-call(bf16[137,8461]{1,0:T(8,128)(2,1)} %bitcast.12, s32[1,96]{1,0:T(1,128)} %bitcast.21, bf16[137,40,128]{2,1,0:T(8,128)(2,1)} %bitcast.13, s32[16,32]{1,0:T(8,128)} %bitcast.20), custom_call_target="tpu_custom_call" | custom-call | tf_op jit(solution)/shard_map/front/pallas_call | solution.py:912
  11.5 0.0 copy-done
  11.5 0.0 copy-done.1
  11.6 0.0 copy-done.2
  11.6 0.0 copy-done.3
  11.6 0.0 copy-done.4
  11.6 0.0 copy-done.5
  11.6 57.1 %conditional.1 = ((f32[96,40,512]{2,1,0:T(8,128)}, bf16[137,40,128]{2,1,0:T(8,128)(2,1)})) conditional(s32[]{:T(128)} %bitcast.4, (bf16[3840,128]{1,0:T(8,128)(2,1)S(1)}, s32[4,16,128]{2,1,0:T(8,128)S(1)}, bf16[137,40,128]{2,1,0:T(8,128)(2,1)S(1)}, bf16[80,80]{1,0:T(8,128)(2,1)S(1)}, bf16[137,128]{1,0:T(8,128)(2,1)S(1)}, ...), branch_computations={%region_0.0_spmd, %region_1.0_spmd} | conditional | bytes 8 | solution.py:1026
  11.6 51.6 %exchange_tight.1 = (bf16[16,960,128]{2,1,0:T(8,128)(2,1)S(1)}, bf16[137,40,128]{2,1,0:T(8,128)(2,1)S(1)}, bf16[512,512]{1,0:T(8,128)(2,1)S(1)}) custom-call(bf16[3840,128]{1,0:T(8,128)(2,1)S(1)} %get-tuple-element.44.owned_ref, s32[4,16,128]{2,1,0:T(8,128)S(1)} %get-tuple-element.45.tables_ref, bf16[137,40,128]{2,1,0:T(8,128)(2,1)S(1)} %get-tuple-element.46.anom_ref, ...), custom_call_target="tpu_custom_call" | custom-call | tf_op jit(solution)/shard_map/cond/branch_1_fun/exchange_tight/pallas_call | solution.py:964
  63.2 5.3 %combine.3 = (f32[96,40,512]{2,1,0:T(8,128)}, bf16[137,40,128]{2,1,0:T(8,128)(2,1)}) custom-call(f32[96]{0:T(128)S(1)} %get-tuple-element.43.bias_ref, bf16[16,960,128]{2,1,0:T(8,128)(2,1)S(1)} %get-tuple-element.51.recv_ref, bf16[512,512]{1,0:T(8,128)(2,1)S(1)} %get-tuple-element.52.spread_ref, bf16[137,40,128]{2,1,0:T(8,128)(2,1)S(1)} %get-tuple-element.53.mixed_ref), custom_call_target="tpu_custom_call" | custom-call | tf_op jit(solution)/shard_map/cond/branch_1_fun/combine/pallas_call | solution.py:999
Async XLA Ops:
  0.6 10.9 %copy-start = (bf16[40,137,128]{2,0,1:T(8,128)(2,1)S(1)}, bf16[40,137,128]{2,0,1:T(8,128)(2,1)}, u32[]{:S(2)}) copy-start(bf16[40,137,128]{2,0,1:T(8,128)(2,1)} %param.12) | copy-start | bytes 4208644
  0.6 10.9 %copy-start.1 = (bf16[137,128]{1,0:T(8,128)(2,1)S(1)}, bf16[137,128]{1,0:T(8,128)(2,1)}, u32[]{:S(2)}) copy-start(bf16[137,128]{1,0:T(8,128)(2,1)} %param.14) | copy-start | bytes 105220
  0.7 10.9 %copy-start.2 = (bf16[1,80,80]{2,1,0:T(8,128)(2,1)S(1)}, bf16[1,80,80]{2,1,0:T(8,128)(2,1)}, u32[]{:S(2)}) copy-start(bf16[1,80,80]{2,1,0:T(8,128)(2,1)} %param.13) | copy-start | bytes 38404
  0.7 10.9 %copy-start.3 = (s32[512,4]{0,1:T(4,128)S(1)}, s32[512,4]{0,1:T(4,128)}, u32[]{:S(2)}) copy-start(s32[512,4]{0,1:T(4,128)} %param.19) | copy-start | bytes 24580
  0.7 10.9 %copy-start.4 = (bf16[512,4]{0,1:T(4,128)(2,1)S(1)}, bf16[512,4]{0,1:T(4,128)(2,1)}, u32[]{:S(2)}) copy-start(bf16[512,4]{0,1:T(4,128)(2,1)} %param.20) | copy-start | bytes 12292
  0.7 10.9 %copy-start.5 = (f32[96]{0:T(128)S(1)}, f32[96]{0:T(128)}, u32[]{:S(2)}) copy-start(f32[96]{0:T(128)} %param.21) | copy-start | bytes 1156
